TPU v7x, 32 devices: a whole 2x2x4 slice. The times are simulated.
32 devices in a mesh: uly: 2 (over y), blk: 16 (over z, x, core).
Axes of the slice: x: 2, y: 2, z: 4, core: 2. Of those that a mesh axis runs over, the one named last changes fastest.
Arguments:
- query_inputs: bfloat16 [4096, 2048], P(('blk', 'uly')), may hold values from -6 to 6
- key_inputs: bfloat16 [4096, 1024], P(('blk', 'uly')), may hold values from -6 to 6
- value_inputs: bfloat16 [4096, 1024], P(('blk', 'uly')), may hold values from -6 to 6
- forward_out: bfloat16 [4096, 2048], P(('blk', 'uly')), may hold values from -6 to 6
- output_gradient: bfloat16 [4096, 2048], P(('blk', 'uly')), may hold values from -4 to 4
- lse_parts: float32 [4096, 16, 2], P(('blk', 'uly')), may hold values from 3 to 247
- segment_ids: int32 [4096], P(('blk', 'uly')), may hold values from 0 to 31, never falling along the last dimension, each value on 1 to 512 neighbouring positions
Outputs:
- query_grad: bfloat16 [4096, 2048], P(('blk', 'uly'))
- key_grad: bfloat16 [4096, 1024], P(('blk', 'uly'))
- value_grad: bfloat16 [4096, 1024], P(('blk', 'uly'))
Inputs may be any that keep to these rules, and one draw needn't show every extreme that they name: `segment_ids`: never falls along the sequence; every document holds 1 to 512 tokens, and some document exactly 512.
All inputs are finite; a program needn't handle non-finite values.
Results may differ from a plain program's by a relative error of at most 0.0051.
Values may be sent and summed in bfloat16 or wider, within the bound.
A program may use at most 128 MiB of HBM per device.

v0:
```python
import functools
import math

import jax
import jax.numpy as jnp
from jax import lax
from jax.experimental import pallas as pl
from jax.experimental.pallas import tpu as pltpu
from jax.sharding import PartitionSpec as P

HEAD_SIZE = 128
QUERY_HEADS = 16
KEY_VALUE_HEADS = 8
GROUP = QUERY_HEADS // KEY_VALUE_HEADS
TILE = 256
PIECES = 2
FAR = -1e30


def dot_nt(a, b):
    return lax.dot_general(a, b, (((1,), (1,)), ((), ())), preferred_element_type=jnp.float32)


def dot_nn(a, b):
    return lax.dot_general(a, b, (((1,), (0,)), ((), ())), preferred_element_type=jnp.float32)


def dot_tn(a, b):
    return lax.dot_general(a, b, (((0,), (0,)), ((), ())), preferred_element_type=jnp.float32)


def kernel(
    uly_count, blk_count,
    q_ref, do_hbm, k_hbm, v_hbm, out_hbm, lp_hbm, ids_hbm,
    dq_ref, dk_ref, dv_ref,
    qb, dob, kvb, statb, idb, bias,
    dqacc, acc0, acc2, dqs, ret1, ret2, in1, in2, dkvs,
    do_ref, k_ref, v_ref, out_ref, lp_ref, ids_ref, stat_ref,
    loc_sem, keep_sem,
    kv_s, kv_r, qd_s, qd_r, st_s, st_r, id_s, id_r,
    h2_s, h2_r, h2i_s, h2i_r, pt_s, pt_r, pti_s, pti_r,
    r1_s, r1_r, r2_s, r2_r, oq_s, oq_r, okv_s, okv_r,
):
    U, B = uly_count, blk_count
    T = q_ref.shape[0]
    R = T * U
    KH = KEY_VALUE_HEADS // U
    D = HEAD_SIZE
    GD = GROUP * D
    scale = 1.0 / math.sqrt(D)
    u = lax.axis_index("uly")
    b = lax.axis_index("blk")
    odd = lax.rem(b, 2)
    even = odd == 0
    mate = b + 1 - 2 * odd

    def at(blk, uly):
        return {"blk": blk, "uly": uly}

    def rcopy(src, dst, ssem, rsem, dev):
        return pltpu.make_async_remote_copy(
            src_ref=src, dst_ref=dst, send_sem=ssem, recv_sem=rsem,
            device_id=dev, device_id_type=pl.DeviceIdType.MESH,
        )

    def cols(first, width):
        return pl.ds(pl.multiple_of(first, 128), width)

    def rows(place):
        return pl.ds(pl.multiple_of(place * T, T), T)

    has_up2 = b + 2 < B
    has_down2 = b >= 2
    sends_mate = jnp.logical_or(even, b >= 3)

    loads = [
        pltpu.make_async_copy(src, dst, loc_sem.at[5 + i])
        for i, (src, dst) in enumerate([
            (ids_hbm, ids_ref), (k_hbm, k_ref), (v_hbm, v_ref),
            (do_hbm, do_ref), (out_hbm, out_ref), (lp_hbm, lp_ref),
        ])
    ]
    own_kv = [
        pltpu.make_async_copy(
            k_hbm.at[:, cols(u * KH * D, KH * D)], kvb.at[0, 0, rows(u), :], loc_sem.at[2]
        ),
        pltpu.make_async_copy(
            v_hbm.at[:, cols(u * KH * D, KH * D)], kvb.at[0, 1, rows(u), :], loc_sem.at[3]
        ),
    ]
    for copy in own_kv + loads:
        copy.start()

    barrier = pltpu.get_barrier_semaphore()
    for k in range(1, U):
        pl.semaphore_signal(
            barrier, inc=1, device_id=at(b, lax.rem(u + k, U)), device_id_type=pl.DeviceIdType.MESH
        )
    pl.semaphore_signal(barrier, inc=1, device_id=at(mate, u), device_id_type=pl.DeviceIdType.MESH)

    @pl.when(has_up2)
    def _():
        pl.semaphore_signal(
            barrier, inc=1, device_id=at(b + 2, u), device_id_type=pl.DeviceIdType.MESH
        )

    @pl.when(has_down2)
    def _():
        pl.semaphore_signal(
            barrier, inc=1, device_id=at(b - 2, u), device_id_type=pl.DeviceIdType.MESH
        )

    expected = U + has_up2.astype(jnp.int32) + has_down2.astype(jnp.int32)
    pl.semaphore_wait(barrier, expected)

    own_q = [
        pltpu.make_async_copy(
            q_ref.at[:, cols(u * KH * GD, KH * GD)], qb.at[rows(u), :], loc_sem.at[0]
        ),
        pltpu.make_async_copy(
            do_hbm.at[:, cols(u * KH * GD, KH * GD)], dob.at[rows(u), :], loc_sem.at[1]
        ),
    ]
    own_id = pltpu.make_async_copy(ids_hbm, idb.at[0, u], loc_sem.at[4])

    def id_in(k, place, dev):
        return rcopy(ids_ref, idb.at[0, place], id_s.at[k - 1], id_r.at[k - 1], dev)

    def st_in(k, place, peer, dev):
        return rcopy(stat_ref.at[peer], statb.at[place], st_s.at[k - 1], st_r.at[k - 1], dev)

    def kv_in(k, which, j, place, peer, dev):
        ref = (k_ref, v_ref)[which]
        return rcopy(
            ref.at[:, cols((peer * KH + j) * D, D)],
            kvb.at[0, which, rows(place), cols(j * D, D)],
            kv_s.at[which, j, k - 1], kv_r.at[which, j, k - 1], dev,
        )

    def qd_in(k, which, j, place, peer, dev):
        ref, buf = ((q_ref, qb), (do_ref, dob))[which]
        return rcopy(
            ref.at[:, cols((peer * KH + j) * GD, GD)],
            buf.at[rows(place), cols(j * GD, GD)],
            qd_s.at[which, j, k - 1], qd_r.at[which, j, k - 1], dev,
        )

    def h2(j, i, place):
        return rcopy(
            kvb.at[0, :, rows(place), cols(j * D, D)], kvb.at[2, :, rows(place), cols(j * D, D)],
            h2_s.at[j, i], h2_r.at[j, i], at(b + 2, u),
        )

    peers = [(k, lax.rem(u + k, U), lax.rem(u + U - k, U)) for k in range(1, U)]
    shares = [(0, u)] + [(k, frm) for k, _, frm in peers]
    for copy in own_kv:
        copy.wait()

    @pl.when(has_up2)
    def _():
        for j in range(KH):
            h2(j, 0, u).start()

    loads[0].wait()
    for k, to, _ in peers:
        id_in(k, u, at(b, to)).start()
    loads[1].wait()
    loads[2].wait()
    for j in range(KH):
        for k, to, _ in peers:
            for which in range(2):
                kv_in(k, which, j, u, to, at(b, to)).start()
    for copy in [own_id] + own_q:
        copy.start()

    for copy in loads[3:]:
        copy.wait()
    G = KH * GROUP
    lane = lax.broadcasted_iota(jnp.int32, (T, 128), 1)
    table = jnp.zeros((T, 128), jnp.float32)
    for h in range(U * G):
        piece = slice(h * D, (h + 1) * D)
        total = jnp.sum(
            do_ref[:, piece].astype(jnp.float32) * out_ref[:, piece].astype(jnp.float32),
            axis=1, keepdims=True,
        )
        table = jnp.where(lane == h, total, table)
    table = table.T
    part0, part1 = lp_ref[:, 0, :], lp_ref[:, 1, :]
    highest = jnp.maximum(part0, part1)
    lse_rows = highest + jnp.log(jnp.exp(part0 - highest) + jnp.exp(part1 - highest))
    for p in range(U):
        stat_ref[p, :G, :] = lse_rows[p * G:(p + 1) * G]
        stat_ref[p, G:2 * G, :] = table[p * G:(p + 1) * G]
    statb[u] = stat_ref[u]

    for j in range(KH):
        for k, to, _ in peers:
            for which in range(2):
                qd_in(k, which, j, u, to, at(b, to)).start()
        if j == 0:
            for k, to, _ in peers:
                st_in(k, u, to, at(b, to)).start()


    def h2id():
        return rcopy(idb.at[0], idb.at[2], h2i_s.at[0], h2i_r.at[0], at(b + 2, u))

    def pt(j):
        return rcopy(
            kvb.at[2 * odd, :, :, cols(j * D, D)], kvb.at[1, :, :, cols(j * D, D)],
            pt_s.at[j], pt_r.at[j], at(mate, u),
        )

    def ptid():
        return rcopy(idb.at[2 * odd], idb.at[1], pti_s.at[0], pti_r.at[0], at(mate, u))

    own_id.wait()
    for k, _, frm in peers:
        id_in(k, frm, at(b, frm)).wait_recv()

    @pl.when(has_up2)
    def _():
        h2id().start()

    @pl.when(even)
    def _():
        ptid().start()

    for j in range(KH):
        for k, _, frm in peers:
            for which in range(2):
                kv_in(k, which, j, frm, frm, at(b, frm)).wait_recv()

        @pl.when(has_up2)
        def _():
            for k, _, frm in peers:
                h2(j, k, frm).start()

        @pl.when(even)
        def _():
            pt(j).start()

    def make_bias(hop):
        for kp in range(U):
            key_ids = jnp.broadcast_to(idb[hop, kp, 0:1, :].astype(jnp.float32), (T, T)).T
            for qp in range(U):
                query_ids = idb[0, qp, 0:1, :].astype(jnp.float32)
                good = key_ids == query_ids
                if hop == 0:
                    kpos = lax.broadcasted_iota(jnp.int32, (T, T), 0) + kp * T
                    qpos = lax.broadcasted_iota(jnp.int32, (T, T), 1) + qp * T
                    good = jnp.logical_and(good, kpos <= qpos)
                bias[hop, kp * T:(kp + 1) * T, qp * T:(qp + 1) * T] = jnp.where(good, 0.0, FAR)

    make_bias(0)

    @pl.when(has_down2)
    def _():
        h2id().wait_recv()
        make_bias(2)

        @pl.when(odd == 1)
        def _():
            ptid().start()

    def arrive2(j):
        @pl.when(has_down2)
        def _():
            for i, place in shares:
                h2(j, i, place).wait_recv()

            @pl.when(odd == 1)
            def _():
                pt(j).start()

    arrive2(0)

    @pl.when(b >= 1)
    def _():
        ptid().wait_recv()
        make_bias(1)

    for copy in own_q:
        copy.wait()
    for k, _, frm in peers:
        st_in(k, frm, frm, at(b, frm)).wait_recv()

    tile = min(TILE, R)
    steps = R // tile
    per = tile // T if tile >= T else 1

    def stat_row(row, qt):
        parts = [statb[qt * per + i, pl.ds(row, 1), :] for i in range(per)]
        return parts[0] if per == 1 else jnp.concatenate(parts, axis=1)

    def hop_grads(hop, j, acc):
        def key_step(kt, _):
            krow = pl.ds(pl.multiple_of(kt * tile, tile), tile)
            kc = kvb[hop, 0, krow, cols(j * D, D)]
            vc = kvb[hop, 1, krow, cols(j * D, D)]

            def query_step(qt, carry):
                dk, dv = carry
                qrow = pl.ds(pl.multiple_of(qt * tile, tile), tile)
                for g in range(GROUP):
                    qc = qb[qrow, cols(j * GD + g * D, D)]
                    dc = dob[qrow, cols(j * GD + g * D, D)]
                    head = j * GROUP + g
                    lse = stat_row(head, qt)
                    delta = stat_row(G + head, qt)
                    w = jnp.exp(dot_nt(kc, qc) * scale - lse + bias[hop, krow, pl.ds(pl.multiple_of(qt * tile, tile), tile)])
                    dv = dv + dot_nn(w.astype(jnp.bfloat16), dc)
                    ds = (w * (dot_nt(vc, dc) - delta)).astype(jnp.bfloat16)
                    dk = dk + dot_nn(ds, qc)
                    part = dot_tn(ds, kc)
                    dqacc[qrow, g * D:(g + 1) * D] += part
                return dk, dv

            zero = jnp.zeros((tile, D), jnp.float32)
            if steps == 1:
                dk, dv = query_step(0, (zero, zero))
            else:
                dk, dv = lax.fori_loop(0, steps, query_step, (zero, zero))
            acc[j, 0, krow, :] = (dk * scale).astype(acc.dtype)
            acc[j, 1, krow, :] = dv.astype(acc.dtype)
            return 0

        if steps == 1:
            key_step(0, 0)
        else:
            lax.fori_loop(0, steps, key_step, 0)

    def give1(j):
        return rcopy(ret1.at[j], in1.at[j], r1_s.at[j], r1_r.at[j], at(mate, u))

    def give2(j):
        return rcopy(ret2.at[j], in2.at[j], r2_s.at[j], r2_r.at[j], at(b - 2, u))

    def oq(k, j, place, dev):
        return rcopy(
            dqs.at[j, rows(place), :], dq_ref.at[:, cols((u * KH + j) * GD, GD)],
            oq_s.at[j, k - 1], oq_r.at[j, k - 1], dev,
        )

    def okv(k, which, j, place, dev):
        ref = (dk_ref, dv_ref)[which]
        return rcopy(
            dkvs.at[j, which, rows(place), :], ref.at[:, cols((u * KH + j) * D, D)],
            okv_s.at[which, j, k - 1], okv_r.at[which, j, k - 1], dev,
        )

    def keep_q(j):
        return pltpu.make_async_copy(
            dqs.at[j, rows(u), :], dq_ref.at[:, cols((u * KH + j) * GD, GD)], keep_sem.at[2, j]
        )

    def keep_kv(which, j):
        ref = (dk_ref, dv_ref)[which]
        return pltpu.make_async_copy(
            dkvs.at[j, which, rows(u), :], ref.at[:, cols((u * KH + j) * D, D)],
            keep_sem.at[which, j],
        )

    def compute(j):
        for k, _, frm in peers:
            for which in range(2):
                qd_in(k, which, j, frm, frm, at(b, frm)).wait_recv()
        dqacc[...] = jnp.zeros_like(dqacc)

        @pl.when(b >= 1)
        def _():
            pt(j).wait_recv()
            hop_grads(1, j, ret1)
            give1(j).start()

        @pl.when(has_down2)
        def _():
            hop_grads(2, j, acc2)

        stage_a(j)
        hop_grads(0, j, acc0)

        dqs[j] = (dqacc[...] * scale).astype(jnp.bfloat16)
        for k, to, _ in peers:
            oq(k, j, to, at(b, to)).start()
        keep_q(j).start()

    def stage_a(j):
        @pl.when(jnp.logical_and(odd == 1, has_down2))
        def _():
            give1(j).wait_recv()
            ret2[j] = (acc2[j] + in1[j].astype(jnp.float32)).astype(jnp.bfloat16)

        @pl.when(jnp.logical_and(even, has_down2))
        def _():
            ret2[j] = acc2[j].astype(jnp.bfloat16)

        @pl.when(has_down2)
        def _():
            give2(j).start()

    def stage_b(j):
        @pl.when(even)
        def _():
            give1(j).wait_recv()
            acc0[j] += in1[j].astype(jnp.float32)

        @pl.when(has_up2)
        def _():
            give2(j).wait_recv()
            acc0[j] += in2[j].astype(jnp.float32)

        dkvs[j] = acc0[j].astype(jnp.bfloat16)
        for k, to, _ in peers:
            for which in range(2):
                okv(k, which, j, to, at(b, to)).start()
        for which in range(2):
            keep_kv(which, j).start()

    def head_step(j, _):
        @pl.when(j + 1 < KH)
        def _():
            arrive2(jnp.minimum(j + 1, KH - 1))

        compute(j)

        @pl.when(j >= 2)
        def _():
            stage_b(jnp.maximum(j - 2, 0))

        return 0

    lax.fori_loop(0, KH, head_step, 0)
    if KH >= 2:
        stage_b(KH - 2)
    stage_b(KH - 1)

    for k, to, frm in peers:
        id_in(k, u, at(b, to)).wait_send()
        st_in(k, u, to, at(b, to)).wait_send()

    @pl.when(has_up2)
    def _():
        h2id().wait_send()

    @pl.when(sends_mate)
    def _():
        ptid().wait_send()

    def finish(j, _):
        keep_q(j).wait()
        for which in range(2):
            keep_kv(which, j).wait()
        for k, to, frm in peers:
            for which in range(2):
                kv_in(k, which, j, u, to, at(b, to)).wait_send()
                qd_in(k, which, j, u, to, at(b, to)).wait_send()

        @pl.when(has_up2)
        def _():
            for i, place in shares:
                h2(j, i, place).wait_send()

        @pl.when(sends_mate)
        def _():
            pt(j).wait_send()

        @pl.when(b >= 1)
        def _():
            give1(j).wait_send()

        @pl.when(has_down2)
        def _():
            give2(j).wait_send()

        for k, to, frm in peers:
            oq(k, j, to, at(b, to)).wait_send()
            for which in range(2):
                okv(k, which, j, to, at(b, to)).wait_send()
            rcopy(
                dqs.at[j, rows(frm), :], dq_ref.at[:, cols((frm * KH + j) * GD, GD)],
                oq_s.at[j, k - 1], oq_r.at[j, k - 1], at(b, frm),
            ).wait_recv()
            for which in range(2):
                ref = (dk_ref, dv_ref)[which]
                rcopy(
                    dkvs.at[j, which, rows(frm), :], ref.at[:, cols((frm * KH + j) * D, D)],
                    okv_s.at[which, j, k - 1], okv_r.at[which, j, k - 1], at(b, frm),
                ).wait_recv()
        return 0

    lax.fori_loop(0, KH, finish, 0)


def close_kernel(a_in, b_in, c_in, a_out, b_out, c_out, a_mid, b_mid, c_mid, in_sem, out_sem):
    moves = []
    for i, (src, mid, dst) in enumerate(
        [(a_in, a_mid, a_out), (b_in, b_mid, b_out), (c_in, c_mid, c_out)]
    ):
        height = src.shape[0] // PIECES
        for n in range(PIECES):
            part = pl.ds(n * height, height)
            moves.append((
                pltpu.make_async_copy(src.at[part], mid.at[part], in_sem.at[i, n]),
                pltpu.make_async_copy(mid.at[part], dst.at[part], out_sem.at[i, n]),
            ))
    for load, _ in moves:
        load.start()
    for load, store in moves:
        load.wait()
        store.start()
    for _, store in moves:
        store.wait()


def per_device(uly_count, blk_count, q, k, v, out, grad, lse_parts, segment_ids):
    U, B = uly_count, blk_count
    T = q.shape[0]
    R = T * U
    KH = KEY_VALUE_HEADS // U
    G = KH * GROUP
    D = HEAD_SIZE
    stat_rows = -(-2 * G // 8) * 8
    parts = lse_parts.transpose(1, 2, 0)
    ids = segment_ids.reshape(1, T)
    bf, f32 = jnp.bfloat16, jnp.float32
    n = max(U - 1, 1)
    dma = pltpu.SemaphoreType.DMA
    sems = []
    for shape in [(2, KH, n), (2, KH, n), (n,), (n,), (KH, U), (1,), (KH,), (1,), (KH,), (KH,), (KH, n), (2, KH, n)]:
        sems += [dma(shape), dma(shape)]
    vm = pltpu.VMEM
    results = pl.pallas_call(
        functools.partial(kernel, U, B),
        out_shape=(
            jax.ShapeDtypeStruct(q.shape, bf),
            jax.ShapeDtypeStruct(k.shape, bf),
            jax.ShapeDtypeStruct(v.shape, bf),
        ),
        in_specs=[pl.BlockSpec(memory_space=pltpu.HBM)] * 7,
        out_specs=tuple([pl.BlockSpec(memory_space=pltpu.HBM)] * 3),
        scratch_shapes=[
            vm((R, G * D), bf),
            vm((R, G * D), bf),
            vm((3, 2, R, KH * D), bf),
            vm((U, stat_rows, T), f32),
            vm((3, U, 1, T), jnp.int32),
            vm((3, R, R), f32),
            vm((R, GROUP * D), f32),
            vm((KH, 2, R, D), f32),
            vm((KH, 2, R, D), f32),
            vm((KH, R, GROUP * D), bf),
            vm((KH, 2, R, D), bf),
            vm((KH, 2, R, D), bf),
            vm((KH, 2, R, D), bf),
            vm((KH, 2, R, D), bf),
            vm((KH, 2, R, D), bf),
            vm(q.shape, bf),
            vm(k.shape, bf),
            vm(v.shape, bf),
            vm(q.shape, bf),
            vm(parts.shape, f32),
            vm((1, T), jnp.int32),
            vm((U, stat_rows, T), f32),
            dma((11,)),
            dma((3, KH)),
        ] + sems,
        compiler_params=pltpu.CompilerParams(
            collective_id=0, has_side_effects=True, vmem_limit_bytes=56 << 20
        ),
    )(q, grad, k, v, out, parts, ids)
    hbm = [pl.BlockSpec(memory_space=pltpu.HBM)] * 3
    return pl.pallas_call(
        close_kernel,
        out_shape=tuple(jax.ShapeDtypeStruct(r.shape, r.dtype) for r in results),
        in_specs=hbm,
        out_specs=tuple(hbm),
        scratch_shapes=[vm(r.shape, r.dtype) for r in results]
        + [dma((3, PIECES)), dma((3, PIECES))],
        compiler_params=pltpu.CompilerParams(vmem_limit_bytes=56 << 20),
    )(*results)


def solution(mesh):
    spec = P(("blk", "uly"), None)
    body = functools.partial(per_device, mesh.shape["uly"], mesh.shape["blk"])
    return jax.shard_map(
        body,
        mesh=mesh,
        in_specs=(spec, spec, spec, spec, spec, P(("blk", "uly"), None, None), P(("blk", "uly"))),
        out_specs=(spec, spec, spec),
        check_vma=False,
    )
```

profile of v0, /device:TPU:0, one launch (start us, length us, event | category | flops | bytes accessed | tf_op | source)
XLA Modules:
  0.0 37.4 jit_solution(17696400663080791951)
XLA Ops:
  0.6 34.7 %shard_map.94 = (bf16[128,2048]{1,0:T(8,128)(2,1)}, bf16[128,1024]{1,0:T(8,128)(2,1)}, bf16[128,1024]{1,0:T(8,128)(2,1)}) custom-call(bf16[128,2048]{1,0:T(8,128)(2,1)} %q_ref.1, bf16[128,2048]{1,0:T(8,128)(2,1)} %do_hbm.1, bf16[128,1024]{1,0:T(8,128)(2,1)} %k_hbm.1, bf16[128,1024]{1,0:T(8,128)(2,1)} %v_hbm.1, bf16[128,2048]{1,0:T(8,128)(2,1)} %out_hbm.1, ...), custom_call_target="tpu_custom_call" | custom-call | tf_op jit(solution)/shard_map/pallas_call | solution.py:534
  35.4 2.0 %shard_map.95 = (bf16[128,2048]{1,0:T(8,128)(2,1)}, bf16[128,1024]{1,0:T(8,128)(2,1)}, bf16[128,1024]{1,0:T(8,128)(2,1)}) custom-call(bf16[128,2048]{1,0:T(8,128)(2,1)} %get-tuple-element.6.a_in, bf16[128,1024]{1,0:T(8,128)(2,1)} %get-tuple-element.7.b_in, bf16[128,1024]{1,0:T(8,128)(2,1)} %get-tuple-element.8.c_in), custom_call_target="tpu_custom_call" | custom-call | tf_op jit(solution)/shard_map/pallas_call | solution.py:574
where the time goes:
time: 37.5 us; the launch traced here: 37.4 us
  Pallas kernels  36.7 us (98%)
  between operations  0.64 us (2%)
    pallas_call x1, Pallas kernels, per_device(): pl.pallas_call(functools.partial(kernel, U, B), out_shape=(jax.ShapeDtype...  34.7 us
    pallas_call x1, Pallas kernels, per_device(): pl.pallas_call(close_kernel, out_shape=tuple((jax.ShapeDtypeStruct(r.shap...  2.01 us

commit v1 on v0

v1 whole, which is shorter than its diff:
```python
import functools
import math

import jax
import jax.numpy as jnp
from jax import lax
from jax.experimental import pallas as pl
from jax.experimental.pallas import tpu as pltpu
from jax.sharding import PartitionSpec as P

HEAD_SIZE = 128
QUERY_HEADS = 16
KEY_VALUE_HEADS = 8
GROUP = QUERY_HEADS // KEY_VALUE_HEADS
TILE = 256
FAR = -1e30


def dot_nt(a, b):
    return lax.dot_general(a, b, (((1,), (1,)), ((), ())), preferred_element_type=jnp.float32)


def dot_nn(a, b):
    return lax.dot_general(a, b, (((1,), (0,)), ((), ())), preferred_element_type=jnp.float32)


def dot_tn(a, b):
    return lax.dot_general(a, b, (((0,), (0,)), ((), ())), preferred_element_type=jnp.float32)


def kernel(
    uly_count, blk_count,
    q_hbm, do_hbm, k_hbm, v_hbm, out_hbm, lp_hbm, ids_hbm,
    dq_ref, dkv_ref,
    qdb, kvb, statb, idb, bias,
    dqacc, acc0, acc2, dqs, ret1, ret2, in1, in2, dkvs,
    do_ref, kv_ref, out_ref, lp_ref, ids_ref, stat_ref,
    loc_sem,
    kv_s, kv_r, qd_s, qd_r, st_s, st_r, id_s, id_r,
    h2_s, h2_r, h2i_s, h2i_r, pt_s, pt_r, pti_s, pti_r,
    r1_s, r1_r, r2_s, r2_r, oq_s, oq_r, okv_s, okv_r,
):
    U, B = uly_count, blk_count
    T = q_hbm.shape[0]
    R = T * U
    KH = KEY_VALUE_HEADS // U
    D = HEAD_SIZE
    GD = GROUP * D
    G = KH * GROUP
    scale = 1.0 / math.sqrt(D)
    u = lax.axis_index("uly")
    b = lax.axis_index("blk")
    odd = lax.rem(b, 2)
    even = odd == 0
    mate = b + 1 - 2 * odd

    def at(blk, uly):
        return {"blk": blk, "uly": uly}

    def rcopy(src, dst, ssem, rsem, dev):
        return pltpu.make_async_remote_copy(
            src_ref=src, dst_ref=dst, send_sem=ssem, recv_sem=rsem,
            device_id=dev, device_id_type=pl.DeviceIdType.MESH,
        )

    def cols(first, width):
        return pl.ds(pl.multiple_of(first, 128), width)

    def rows(place):
        return pl.ds(pl.multiple_of(place * T, T), T)

    has_up2 = b + 2 < B
    has_down2 = b >= 2
    sends_mate = jnp.logical_or(even, b >= 3)

    def load(src, dst, sem):
        return pltpu.make_async_copy(src, dst, loc_sem.at[sem])

    own_cols = cols(u * KH * D, KH * D)
    own_kv = [
        load(src.at[:, own_cols], kvb.at[0, i, rows(u), :], 0)
        for i, src in enumerate((k_hbm, v_hbm))
    ]
    load_ids = load(ids_hbm, ids_ref, 1)
    load_kv = [load(src, kv_ref.at[i], 2) for i, src in enumerate((k_hbm, v_hbm))]
    load_do = load(do_hbm, do_ref, 3)
    load_out = load(out_hbm, out_ref, 4)
    load_lp = load(lp_hbm, lp_ref, 5)
    for copy in own_kv + [load_ids] + load_kv + [load_do, load_out, load_lp]:
        copy.start()

    barrier = pltpu.get_barrier_semaphore()
    for k in range(1, U):
        pl.semaphore_signal(
            barrier, inc=1, device_id=at(b, lax.rem(u + k, U)), device_id_type=pl.DeviceIdType.MESH
        )
    pl.semaphore_signal(barrier, inc=1, device_id=at(mate, u), device_id_type=pl.DeviceIdType.MESH)

    @pl.when(has_up2)
    def _():
        pl.semaphore_signal(
            barrier, inc=1, device_id=at(b + 2, u), device_id_type=pl.DeviceIdType.MESH
        )

    @pl.when(has_down2)
    def _():
        pl.semaphore_signal(
            barrier, inc=1, device_id=at(b - 2, u), device_id_type=pl.DeviceIdType.MESH
        )

    expected = U + has_up2.astype(jnp.int32) + has_down2.astype(jnp.int32)
    pl.semaphore_wait(barrier, expected)

    own_q = [
        load(src.at[:, cols(u * KH * GD, KH * GD)], qdb.at[i, rows(u), :], 6)
        for i, src in enumerate((q_hbm, do_hbm))
    ]
    own_id = load(ids_hbm, idb.at[0, u], 7)

    def id_in(k, place, dev):
        return rcopy(ids_ref, idb.at[0, place], id_s.at[k - 1], id_r.at[k - 1], dev)

    def st_in(k, place, peer, dev):
        return rcopy(stat_ref.at[peer], statb.at[place], st_s.at[k - 1], st_r.at[k - 1], dev)

    def kv_in(k, j, place, peer, dev):
        return rcopy(
            kv_ref.at[:, :, cols((peer * KH + j) * D, D)],
            kvb.at[0, :, rows(place), cols(j * D, D)],
            kv_s.at[k - 1], kv_r.at[j, k - 1], dev,
        )

    def qd_in(k, which, j, place, peer, dev):
        ref = (q_hbm, do_ref)[which]
        return rcopy(
            ref.at[:, cols((peer * KH + j) * GD, GD)],
            qdb.at[which, rows(place), cols(j * GD, GD)],
            qd_s.at[which, k - 1], qd_r.at[j, k - 1], dev,
        )

    def await_bytes(ref, sem):
        pltpu.make_async_copy(ref, ref, sem).wait()

    def h2(j, place):
        return rcopy(
            kvb.at[0, :, rows(place), cols(j * D, D)], kvb.at[2, :, rows(place), cols(j * D, D)],
            h2_s.at[0], h2_r.at[j], at(b + 2, u),
        )

    peers = [(k, lax.rem(u + k, U), lax.rem(u + U - k, U)) for k in range(1, U)]
    await_bytes(kvb.at[0, :, rows(u), :], loc_sem.at[0])

    @pl.when(has_up2)
    def _():
        for j in range(KH):
            h2(j, u).start()

    load_ids.wait()
    for k, to, _ in peers:
        id_in(k, u, at(b, to)).start()
    await_bytes(kv_ref, loc_sem.at[2])

    def send_kv(j):
        for k, to, _ in peers:
            kv_in(k, j, u, to, at(b, to)).start()

    def send_qd(j):
        for k, to, _ in peers:
            for which in range(2):
                qd_in(k, which, j, u, to, at(b, to)).start()

    for j in range(min(2, KH)):
        send_kv(j)
    for copy in [own_id] + own_q:
        copy.start()

    load_do.wait()
    load_out.wait()
    load_lp.wait()
    send_qd(0)
    lane = lax.broadcasted_iota(jnp.int32, (T, 128), 1)
    table = jnp.zeros((T, 128), jnp.float32)
    for h in range(U * G):
        piece = slice(h * D, (h + 1) * D)
        total = jnp.sum(
            do_ref[:, piece].astype(jnp.float32) * out_ref[:, piece].astype(jnp.float32),
            axis=1, keepdims=True,
        )
        table = jnp.where(lane == h, total, table)
    table = table.T
    part0, part1 = lp_ref[:, 0, :], lp_ref[:, 1, :]
    highest = jnp.maximum(part0, part1)
    lse_rows = highest + jnp.log(jnp.exp(part0 - highest) + jnp.exp(part1 - highest))
    for p in range(U):
        stat_ref[p, :G, :] = lse_rows[p * G:(p + 1) * G]
        stat_ref[p, G:2 * G, :] = table[p * G:(p + 1) * G]
    statb[u] = stat_ref[u]

    for k, to, _ in peers:
        st_in(k, u, to, at(b, to)).start()
    for j in range(2, KH):
        send_kv(j)
    for j in range(1, KH):
        send_qd(j)

    def h2id():
        return rcopy(idb.at[0], idb.at[2], h2i_s.at[0], h2i_r.at[0], at(b + 2, u))

    def pt(j):
        return rcopy(
            kvb.at[2 * odd, :, :, cols(j * D, D)], kvb.at[1, :, :, cols(j * D, D)],
            pt_s.at[0], pt_r.at[j], at(mate, u),
        )

    def ptid():
        return rcopy(idb.at[2 * odd], idb.at[1], pti_s.at[0], pti_r.at[0], at(mate, u))

    own_id.wait()
    for k, _, frm in peers:
        id_in(k, frm, at(b, frm)).wait_recv()

    @pl.when(has_up2)
    def _():
        h2id().start()

    @pl.when(even)
    def _():
        ptid().start()

    def forward(j):
        for k, _, frm in peers:
            kv_in(k, j, frm, frm, at(b, frm)).wait_recv()

        @pl.when(has_up2)
        def _():
            for k, _, frm in peers:
                h2(j, frm).start()

        @pl.when(even)
        def _():
            pt(j).start()

    def make_bias(hop):
        for kp in range(U):
            key_ids = jnp.broadcast_to(idb[hop, kp, 0:1, :].astype(jnp.float32), (T, T)).T
            for qp in range(U):
                query_ids = idb[0, qp, 0:1, :].astype(jnp.float32)
                good = key_ids == query_ids
                if hop == 0:
                    kpos = lax.broadcasted_iota(jnp.int32, (T, T), 0) + kp * T
                    qpos = lax.broadcasted_iota(jnp.int32, (T, T), 1) + qp * T
                    good = jnp.logical_and(good, kpos <= qpos)
                bias[hop, kp * T:(kp + 1) * T, qp * T:(qp + 1) * T] = jnp.where(good, 0.0, FAR)

    make_bias(0)
    forward(0)
    if KH > 1:
        forward(1)

    @pl.when(has_down2)
    def _():
        h2id().wait_recv()
        make_bias(2)

        @pl.when(odd == 1)
        def _():
            ptid().start()

    def arrive2(j):
        @pl.when(has_down2)
        def _():
            await_bytes(kvb.at[2, :, :, cols(j * D, D)], h2_r.at[j])

            @pl.when(odd == 1)
            def _():
                pt(j).start()

    @pl.when(b >= 1)
    def _():
        ptid().wait_recv()
        make_bias(1)

    await_bytes(qdb.at[:, rows(u), :], loc_sem.at[6])
    for k, _, frm in peers:
        st_in(k, frm, frm, at(b, frm)).wait_recv()
    if KH > 2:
        forward(2)
    arrive2(0)

    tile = min(TILE, R)
    steps = R // tile
    per = tile // T if tile >= T else 1

    def stat_row(row, qt):
        parts = [statb[qt * per + i, pl.ds(row, 1), :] for i in range(per)]
        return parts[0] if per == 1 else jnp.concatenate(parts, axis=1)

    def hop_grads(hop, j, acc):
        def key_step(kt, _):
            krow = pl.ds(pl.multiple_of(kt * tile, tile), tile)
            kc = kvb[hop, 0, krow, cols(j * D, D)]
            vc = kvb[hop, 1, krow, cols(j * D, D)]

            def query_step(qt, carry):
                dk, dv = carry
                qrow = pl.ds(pl.multiple_of(qt * tile, tile), tile)
                for g in range(GROUP):
                    qc = qdb[0, qrow, cols(j * GD + g * D, D)]
                    dc = qdb[1, qrow, cols(j * GD + g * D, D)]
                    head = j * GROUP + g
                    lse = stat_row(head, qt)
                    delta = stat_row(G + head, qt)
                    w = jnp.exp(dot_nt(kc, qc) * scale - lse + bias[hop, krow, qrow])
                    dv = dv + dot_nn(w.astype(jnp.bfloat16), dc)
                    ds = (w * (dot_nt(vc, dc) - delta)).astype(jnp.bfloat16)
                    dk = dk + dot_nn(ds, qc)
                    part = dot_tn(ds, kc)
                    dqacc[qrow, g * D:(g + 1) * D] += part
                return dk, dv

            zero = jnp.zeros((tile, D), jnp.float32)
            if steps == 1:
                dk, dv = query_step(0, (zero, zero))
            else:
                dk, dv = lax.fori_loop(0, steps, query_step, (zero, zero))
            acc[j, 0, krow, :] = (dk * scale).astype(acc.dtype)
            acc[j, 1, krow, :] = dv.astype(acc.dtype)
            return 0

        if steps == 1:
            key_step(0, 0)
        else:
            lax.fori_loop(0, steps, key_step, 0)

    def give1(j):
        return rcopy(ret1.at[j], in1.at[j], r1_s.at[0], r1_r.at[j], at(mate, u))

    def give2(j):
        return rcopy(ret2.at[j], in2.at[j], r2_s.at[0], r2_r.at[j], at(b - 2, u))

    def oq(k, j, place, dev):
        return rcopy(
            dqs.at[j, rows(place), :], dq_ref.at[:, cols((u * KH + j) * GD, GD)],
            oq_s.at[k - 1], oq_r.at[k - 1], dev,
        )

    def okv(k, j, place, dev):
        return rcopy(
            dkvs.at[j, :, rows(place), :], dkv_ref.at[:, :, cols((u * KH + j) * D, D)],
            okv_s.at[k - 1], okv_r.at[k - 1], dev,
        )

    def compute(j):
        for k, _, frm in peers:
            await_bytes(qdb.at[:, rows(frm), cols(j * GD, GD)], qd_r.at[j, k - 1])
        dqacc[...] = jnp.zeros_like(dqacc)

        @pl.when(b >= 1)
        def _():
            pt(j).wait_recv()
            hop_grads(1, j, ret1)
            give1(j).start()

        @pl.when(j + 3 < KH)
        def _():
            forward(jnp.minimum(j + 3, KH - 1))

        @pl.when(j + 1 < KH)
        def _():
            arrive2(jnp.minimum(j + 1, KH - 1))

        @pl.when(has_down2)
        def _():
            hop_grads(2, j, acc2)

        stage_a(j)
        hop_grads(0, j, acc0)

        dqs[j] = (dqacc[...] * scale).astype(jnp.bfloat16)
        for k, to, _ in peers:
            oq(k, j, to, at(b, to)).start()
        dq_ref[:, cols((u * KH + j) * GD, GD)] = dqs[j, rows(u), :]

    def stage_a(j):
        @pl.when(jnp.logical_and(odd == 1, has_down2))
        def _():
            give1(j).wait_recv()
            ret2[j] = (acc2[j] + in1[j].astype(jnp.float32)).astype(jnp.bfloat16)

        @pl.when(jnp.logical_and(even, has_down2))
        def _():
            ret2[j] = acc2[j].astype(jnp.bfloat16)

        @pl.when(has_down2)
        def _():
            give2(j).start()

    def stage_b(j):
        @pl.when(even)
        def _():
            give1(j).wait_recv()
            acc0[j] += in1[j].astype(jnp.float32)

        @pl.when(has_up2)
        def _():
            give2(j).wait_recv()
            acc0[j] += in2[j].astype(jnp.float32)

        dkvs[j] = acc0[j].astype(jnp.bfloat16)
        for k, to, _ in peers:
            okv(k, j, to, at(b, to)).start()
        dkv_ref[:, :, cols((u * KH + j) * D, D)] = dkvs[j, :, rows(u), :]

    def head_step(j, _):
        compute(j)

        @pl.when(j >= 2)
        def _():
            stage_b(jnp.maximum(j - 2, 0))

        return 0

    lax.fori_loop(0, KH, head_step, 0)
    if KH >= 2:
        stage_b(KH - 2)
    stage_b(KH - 1)

    for k, to, _ in peers:
        id_in(k, u, at(b, to)).wait_send()
        st_in(k, u, to, at(b, to)).wait_send()
        await_bytes(kv_ref.at[:, :, cols(to * KH * D, KH * D)], kv_s.at[k - 1])
        for which in range(2):
            await_bytes(qdb.at[which, rows(0), :], qd_s.at[which, k - 1])

    @pl.when(has_up2)
    def _():
        h2id().wait_send()
        await_bytes(kvb.at[0], h2_s.at[0])

    @pl.when(sends_mate)
    def _():
        ptid().wait_send()
        await_bytes(kvb.at[0], pt_s.at[0])

    @pl.when(b >= 1)
    def _():
        await_bytes(ret1, r1_s.at[0])

    @pl.when(has_down2)
    def _():
        await_bytes(ret2, r2_s.at[0])

    for k, to, frm in peers:
        await_bytes(dqs.at[:, rows(to), :], oq_s.at[k - 1])
        await_bytes(dkvs.at[:, :, rows(to), :], okv_s.at[k - 1])
        await_bytes(dq_ref.at[:, cols(frm * KH * GD, KH * GD)], oq_r.at[k - 1])
        await_bytes(dkv_ref.at[:, :, cols(frm * KH * D, KH * D)], okv_r.at[k - 1])


def close_kernel(q_in, kv_in, q_out, k_out, v_out, sem):
    half = q_in.shape[0] // 2
    moves = [
        (q_in.at[pl.ds(0, half)], q_out.at[pl.ds(0, half)]),
        (q_in.at[pl.ds(half, half)], q_out.at[pl.ds(half, half)]),
        (kv_in.at[0], k_out),
        (kv_in.at[1], v_out),
    ]
    copies = [pltpu.make_async_copy(src, dst, sem.at[i]) for i, (src, dst) in enumerate(moves)]
    for copy in copies:
        copy.start()
    for copy in copies:
        copy.wait()


def per_device(uly_count, blk_count, q, k, v, out, grad, lse_parts, segment_ids):
    U, B = uly_count, blk_count
    T = q.shape[0]
    R = T * U
    KH = KEY_VALUE_HEADS // U
    G = KH * GROUP
    D = HEAD_SIZE
    stat_rows = -(-2 * G // 8) * 8
    parts = lse_parts.transpose(1, 2, 0)
    ids = segment_ids.reshape(1, T)
    bf, f32 = jnp.bfloat16, jnp.float32
    n = max(U - 1, 1)
    dma = pltpu.SemaphoreType.DMA
    sems = []
    for send, recv in [
        ((n,), (KH, n)), ((2, n), (KH, n)), ((n,), (n,)), ((n,), (n,)),
        ((1,), (KH,)), ((1,), (1,)), ((1,), (KH,)), ((1,), (1,)),
        ((1,), (KH,)), ((1,), (KH,)), ((n,), (n,)), ((n,), (n,)),
    ]:
        sems += [dma(send), dma(recv)]
    vm = pltpu.VMEM
    in_vmem = pl.BlockSpec(memory_space=pltpu.VMEM)
    in_hbm = pl.BlockSpec(memory_space=pltpu.HBM)
    results = pl.pallas_call(
        functools.partial(kernel, U, B),
        out_shape=(vm(q.shape, bf), vm((2,) + k.shape, bf)),
        in_specs=[in_hbm] * 7,
        out_specs=(in_vmem, in_vmem),
        scratch_shapes=[
            vm((2, R, G * D), bf),
            vm((3, 2, R, KH * D), bf),
            vm((U, stat_rows, T), f32),
            vm((3, U, 1, T), jnp.int32),
            vm((3, R, R), f32),
            vm((R, GROUP * D), f32),
            vm((KH, 2, R, D), f32),
            vm((KH, 2, R, D), f32),
            vm((KH, R, GROUP * D), bf),
            vm((KH, 2, R, D), bf),
            vm((KH, 2, R, D), bf),
            vm((KH, 2, R, D), bf),
            vm((KH, 2, R, D), bf),
            vm((KH, 2, R, D), bf),
            vm(q.shape, bf),
            vm((2,) + k.shape, bf),
            vm(q.shape, bf),
            vm(parts.shape, f32),
            vm((1, T), jnp.int32),
            vm((U, stat_rows, T), f32),
            dma((8,)),
        ] + sems,
        compiler_params=pltpu.CompilerParams(
            collective_id=0, has_side_effects=True, vmem_limit_bytes=56 << 20
        ),
    )(q, grad, k, v, out, parts, ids)
    results = [pltpu.with_memory_space_constraint(r, pltpu.VMEM) for r in results]
    return pl.pallas_call(
        close_kernel,
        out_shape=tuple(jax.ShapeDtypeStruct(r.shape, r.dtype) for r in (q, k, v)),
        in_specs=[in_vmem] * 2,
        out_specs=(in_hbm,) * 3,
        scratch_shapes=[dma((4,))],
        compiler_params=pltpu.CompilerParams(vmem_limit_bytes=8 << 20),
    )(*results)


def solution(mesh):
    spec = P(("blk", "uly"), None)
    body = functools.partial(per_device, mesh.shape["uly"], mesh.shape["blk"])
    return jax.shard_map(
        body,
        mesh=mesh,
        in_specs=(spec, spec, spec, spec, spec, P(("blk", "uly"), None, None), P(("blk", "uly"))),
        out_specs=(spec, spec, spec),
        check_vma=False,
    )
```

time: 37.5 us -> 35.6 us (0.949)
  Pallas kernels: 36.7 us -> 34.8 us
    pallas_call x1, Pallas kernels: 2.01 us -> 1 us  [per_device(): pl.pallas_call(close_kernel, out_shape=tuple((jax.ShapeDtypeStruct(r.shap...]
    pallas_call x1, Pallas kernels: 34.7 us -> 33.8 us  [per_device(): pl.pallas_call(functools.partial(kernel, U, B), out_shape=(vm(q.shape, bf...]
where the time goes in v1:
time: 35.6 us; the launch traced here: 35.5 us
  Pallas kernels  34.8 us (98%)
  between operations  0.64 us (2%)
    pallas_call x1, Pallas kernels, per_device(): pl.pallas_call(functools.partial(kernel, U, B), out_shape=(vm(q.shape, bf...  33.8 us
    pallas_call x1, Pallas kernels, per_device(): pl.pallas_call(close_kernel, out_shape=tuple((jax.ShapeDtypeStruct(r.shap...  1 us

profile of v1, /device:TPU:0, one launch (start us, length us, event | category | flops | bytes accessed | tf_op | source)
XLA Modules:
  0.0 35.5 jit_solution(14683907443914095079)
XLA Ops:
  0.6 33.8 %shard_map.94 = (bf16[128,2048]{1,0:T(8,128)(2,1)S(1)}, bf16[2,128,1024]{2,1,0:T(8,128)(2,1)S(1)}) custom-call(bf16[128,2048]{1,0:T(8,128)(2,1)} %q_hbm.1, bf16[128,2048]{1,0:T(8,128)(2,1)} %do_hbm.1, bf16[128,1024]{1,0:T(8,128)(2,1)} %k_hbm.1, bf16[128,1024]{1,0:T(8,128)(2,1)} %v_hbm.1, bf16[128,2048]{1,0:T(8,128)(2,1)} %out_hbm.1, f32[16,2,128]{2,1,0:T(2,128)} %bitcast.2, ...), custom_call_target="tpu_custom_call" | custom-call | tf_op jit(solution)/shard_map/pallas_call | solution.py:498
  34.5 1.0 %shard_map.95 = (bf16[128,2048]{1,0:T(8,128)(2,1)}, bf16[128,1024]{1,0:T(8,128)(2,1)}, bf16[128,1024]{1,0:T(8,128)(2,1)}) custom-call(bf16[128,2048]{1,0:T(8,128)(2,1)S(1)} %get-tuple-element.5.q_in, bf16[2,128,1024]{2,1,0:T(8,128)(2,1)S(1)} %get-tuple-element.6.kv_in), custom_call_target="tpu_custom_call" | custom-call | tf_op jit(solution)/shard_map/pallas_call | solution.py:531

commit v2 on v1

--- a/solution.py
+++ b/solution.py
@@ -14,6 +14,7 @@
 GROUP = QUERY_HEADS // KEY_VALUE_HEADS
 TILE = 256
 FAR = -1e30
+LOG2_E = math.log2(math.e)
 
 
 def dot_nt(a, b):
@@ -35,7 +36,7 @@
     qdb, kvb, statb, idb, bias,
     dqacc, acc0, acc2, dqs, ret1, ret2, in1, in2, dkvs,
     do_ref, kv_ref, out_ref, lp_ref, ids_ref, stat_ref,
-    loc_sem,
+    loc_sem, ready,
     kv_s, kv_r, qd_s, qd_r, st_s, st_r, id_s, id_r,
     h2_s, h2_r, h2i_s, h2i_r, pt_s, pt_r, pti_s, pti_r,
     r1_s, r1_r, r2_s, r2_r, oq_s, oq_r, okv_s, okv_r,
@@ -89,6 +90,7 @@
     for copy in own_kv + [load_ids] + load_kv + [load_do, load_out, load_lp]:
         copy.start()
 
+    first = b < 2
     barrier = pltpu.get_barrier_semaphore()
     for k in range(1, U):
         pl.semaphore_signal(
@@ -102,14 +104,21 @@
             barrier, inc=1, device_id=at(b + 2, u), device_id_type=pl.DeviceIdType.MESH
         )
 
-    @pl.when(has_down2)
+    @pl.when(b >= 4)
     def _():
         pl.semaphore_signal(
             barrier, inc=1, device_id=at(b - 2, u), device_id_type=pl.DeviceIdType.MESH
         )
 
-    expected = U + has_up2.astype(jnp.int32) + has_down2.astype(jnp.int32)
+    met_up2 = jnp.logical_and(has_up2, b >= 2)
+    expected = U + has_down2.astype(jnp.int32) + met_up2.astype(jnp.int32)
     pl.semaphore_wait(barrier, expected)
+
+    @pl.when(jnp.logical_and(has_down2, b < 4))
+    def _():
+        pl.semaphore_signal(
+            ready, inc=1, device_id=at(b - 2, u), device_id_type=pl.DeviceIdType.MESH
+        )
 
     own_q = [
         load(src.at[:, cols(u * KH * GD, KH * GD)], qdb.at[i, rows(u), :], 6)
@@ -150,7 +159,7 @@
     peers = [(k, lax.rem(u + k, U), lax.rem(u + U - k, U)) for k in range(1, U)]
     await_bytes(kvb.at[0, :, rows(u), :], loc_sem.at[0])
 
-    @pl.when(has_up2)
+    @pl.when(met_up2)
     def _():
         for j in range(KH):
             h2(j, u).start()
@@ -192,7 +201,7 @@
     highest = jnp.maximum(part0, part1)
     lse_rows = highest + jnp.log(jnp.exp(part0 - highest) + jnp.exp(part1 - highest))
     for p in range(U):
-        stat_ref[p, :G, :] = lse_rows[p * G:(p + 1) * G]
+        stat_ref[p, :G, :] = lse_rows[p * G:(p + 1) * G] * LOG2_E
         stat_ref[p, G:2 * G, :] = table[p * G:(p + 1) * G]
     statb[u] = stat_ref[u]
 
@@ -202,6 +211,12 @@
         send_kv(j)
     for j in range(1, KH):
         send_qd(j)
+
+    @pl.when(jnp.logical_and(first, has_up2))
+    def _():
+        pl.semaphore_wait(ready, 1)
+        for j in range(KH):
+            h2(j, u).start()
 
     def h2id():
         return rcopy(idb.at[0], idb.at[2], h2i_s.at[0], h2i_r.at[0], at(b + 2, u))
@@ -304,24 +319,29 @@
             def query_step(qt, carry):
                 dk, dv = carry
                 qrow = pl.ds(pl.multiple_of(qt * tile, tile), tile)
+                heads = [cols(j * GD + g * D, D) for g in range(GROUP)]
+                weights, score_grads = [], []
                 for g in range(GROUP):
-                    qc = qdb[0, qrow, cols(j * GD + g * D, D)]
-                    dc = qdb[1, qrow, cols(j * GD + g * D, D)]
-                    head = j * GROUP + g
-                    lse = stat_row(head, qt)
-                    delta = stat_row(G + head, qt)
-                    w = jnp.exp(dot_nt(kc, qc) * scale - lse + bias[hop, krow, qrow])
-                    dv = dv + dot_nn(w.astype(jnp.bfloat16), dc)
-                    ds = (w * (dot_nt(vc, dc) - delta)).astype(jnp.bfloat16)
-                    dk = dk + dot_nn(ds, qc)
-                    part = dot_tn(ds, kc)
-                    dqacc[qrow, g * D:(g + 1) * D] += part
+                    lse = stat_row(j * GROUP + g, qt)
+                    delta = stat_row(G + j * GROUP + g, qt)
+                    w = jnp.exp2(
+                        dot_nt(kc, qdb[0, qrow, heads[g]]) * (scale * LOG2_E) - lse + bias[hop, krow, qrow]
+                    )
+                    ds = w * (dot_nt(vc, qdb[1, qrow, heads[g]]) - delta)
+                    score_grads.append(ds.astype(jnp.bfloat16))
+                    weights.append(w.astype(jnp.bfloat16))
+                queries = jnp.concatenate([qdb[0, qrow, heads[g]] for g in range(GROUP)], axis=0)
+                cotangents = jnp.concatenate([qdb[1, qrow, heads[g]] for g in range(GROUP)], axis=0)
+                dv = dot_nn(jnp.concatenate(weights, axis=1), cotangents) + dv
+                dk = dot_nn(jnp.concatenate(score_grads, axis=1), queries) + dk
+                for g in range(GROUP):
+                    dqacc[qrow, g * D:(g + 1) * D] += dot_tn(score_grads[g], kc)
                 return dk, dv
 
-            zero = jnp.zeros((tile, D), jnp.float32)
             if steps == 1:
-                dk, dv = query_step(0, (zero, zero))
+                dk, dv = query_step(0, (0.0, 0.0))
             else:
+                zero = jnp.zeros((tile, D), jnp.float32)
                 dk, dv = lax.fori_loop(0, steps, query_step, (zero, zero))
             acc[j, 0, krow, :] = (dk * scale).astype(acc.dtype)
             acc[j, 1, krow, :] = dv.astype(acc.dtype)
@@ -522,6 +542,7 @@
             vm((1, T), jnp.int32),
             vm((U, stat_rows, T), f32),
             dma((8,)),
+            pltpu.SemaphoreType.REGULAR,
         ] + sems,
         compiler_params=pltpu.CompilerParams(
             collective_id=0, has_side_effects=True, vmem_limit_bytes=56 << 20

time: 35.6 us -> 35.4 us (level)
  no operation moved by 1% of the time
where the time goes in v2:
time: 35.4 us; the launch traced here: 35.3 us
  Pallas kernels  34.6 us (98%)
  between operations  0.64 us (2%)
    pallas_call x1, Pallas kernels, per_device(): pl.pallas_call(functools.partial(kernel, U, B), out_shape=(vm(q.shape, bf...  33.6 us
    pallas_call x1, Pallas kernels, per_device(): pl.pallas_call(close_kernel, out_shape=tuple((jax.ShapeDtypeStruct(r.shap...  1 us

profile of v2, /device:TPU:0, one launch (start us, length us, event | category | flops | bytes accessed | tf_op | source)
XLA Modules:
  0.0 35.3 jit_solution(360934462007983608)
XLA Ops:
  0.6 33.6 %shard_map.94 = (bf16[128,2048]{1,0:T(8,128)(2,1)S(1)}, bf16[2,128,1024]{2,1,0:T(8,128)(2,1)S(1)}) custom-call(bf16[128,2048]{1,0:T(8,128)(2,1)} %q_hbm.1, bf16[128,2048]{1,0:T(8,128)(2,1)} %do_hbm.1, bf16[128,1024]{1,0:T(8,128)(2,1)} %k_hbm.1, bf16[128,1024]{1,0:T(8,128)(2,1)} %v_hbm.1, bf16[128,2048]{1,0:T(8,128)(2,1)} %out_hbm.1, f32[16,2,128]{2,1,0:T(2,128)} %bitcast.2, ...), custom_call_target="tpu_custom_call" | custom-call | tf_op jit(solution)/shard_map/pallas_call | solution.py:518
  34.3 1.0 %shard_map.95 = (bf16[128,2048]{1,0:T(8,128)(2,1)}, bf16[128,1024]{1,0:T(8,128)(2,1)}, bf16[128,1024]{1,0:T(8,128)(2,1)}) custom-call(bf16[128,2048]{1,0:T(8,128)(2,1)S(1)} %get-tuple-element.5.q_in, bf16[2,128,1024]{2,1,0:T(8,128)(2,1)S(1)} %get-tuple-element.6.kv_in), custom_call_target="tpu_custom_call" | custom-call | tf_op jit(solution)/shard_map/pallas_call | solution.py:552

commit v3 on v2

--- a/solution.py
+++ b/solution.py
@@ -36,7 +36,8 @@
     qdb, kvb, statb, idb, bias,
     dqacc, acc0, acc2, dqs, ret1, ret2, in1, in2, dkvs,
     do_ref, kv_ref, out_ref, lp_ref, ids_ref, stat_ref,
-    loc_sem, ready,
+    q_ref, kx, loc1, part, px, dqt,
+    loc_sem, ready, kx_s, kx_r, px_s, px_r,
     kv_s, kv_r, qd_s, qd_r, st_s, st_r, id_s, id_r,
     h2_s, h2_r, h2i_s, h2i_r, pt_s, pt_r, pti_s, pti_r,
     r1_s, r1_r, r2_s, r2_r, oq_s, oq_r, okv_s, okv_r,
@@ -87,10 +88,12 @@
     load_do = load(do_hbm, do_ref, 3)
     load_out = load(out_hbm, out_ref, 4)
     load_lp = load(lp_hbm, lp_ref, 5)
-    for copy in own_kv + [load_ids] + load_kv + [load_do, load_out, load_lp]:
+    for copy in load_kv + [load_ids] + own_kv + [load_do, load_out, load_lp]:
         copy.start()
 
     first = b < 2
+    alone = jnp.logical_and(b == 0, U == 2)
+    grouped = jnp.logical_not(alone)
     barrier = pltpu.get_barrier_semaphore()
     for k in range(1, U):
         pl.semaphore_signal(
@@ -125,6 +128,7 @@
         for i, src in enumerate((q_hbm, do_hbm))
     ]
     own_id = load(ids_hbm, idb.at[0, u], 7)
+    load_q = load(q_hbm, q_ref, 6)
 
     def id_in(k, place, dev):
         return rcopy(ids_ref, idb.at[0, place], id_s.at[k - 1], id_r.at[k - 1], dev)
@@ -180,13 +184,25 @@
 
     for j in range(min(2, KH)):
         send_kv(j)
-    for copy in [own_id] + own_q:
-        copy.start()
+    own_id.start()
+
+    @pl.when(grouped)
+    def _():
+        for copy in own_q:
+            copy.start()
+
+    @pl.when(alone)
+    def _():
+        load_q.start()
 
     load_do.wait()
     load_out.wait()
     load_lp.wait()
-    send_qd(0)
+
+    @pl.when(grouped)
+    def _():
+        send_qd(0)
+
     lane = lax.broadcasted_iota(jnp.int32, (T, 128), 1)
     table = jnp.zeros((T, 128), jnp.float32)
     for h in range(U * G):
@@ -205,12 +221,28 @@
         stat_ref[p, G:2 * G, :] = table[p * G:(p + 1) * G]
     statb[u] = stat_ref[u]
 
-    for k, to, _ in peers:
-        st_in(k, u, to, at(b, to)).start()
+    @pl.when(grouped)
+    def _():
+        for k, to, _ in peers:
+            st_in(k, u, to, at(b, to)).start()
+
     for j in range(2, KH):
         send_kv(j)
-    for j in range(1, KH):
-        send_qd(j)
+
+    @pl.when(grouped)
+    def _():
+        for j in range(1, KH):
+            send_qd(j)
+
+    def kx_in():
+        return rcopy(kv_ref.at[:, :, pl.ds(0, KH * D)], kx, kx_s.at[0], kx_r.at[0], at(b, 1 - u))
+
+    def px_in():
+        return rcopy(part, px, px_s.at[0], px_r.at[0], at(b, 1 - u))
+
+    @pl.when(jnp.logical_and(alone, u == 0))
+    def _():
+        kx_in().start()
 
     @pl.when(jnp.logical_and(first, has_up2))
     def _():
@@ -295,9 +327,12 @@
         ptid().wait_recv()
         make_bias(1)
 
-    await_bytes(qdb.at[:, rows(u), :], loc_sem.at[6])
-    for k, _, frm in peers:
-        st_in(k, frm, frm, at(b, frm)).wait_recv()
+    @pl.when(grouped)
+    def _():
+        await_bytes(qdb.at[:, rows(u), :], loc_sem.at[6])
+        for k, _, frm in peers:
+            st_in(k, frm, frm, at(b, frm)).wait_recv()
+
     if KH > 2:
         forward(2)
     arrive2(0)
@@ -358,6 +393,12 @@
     def give2(j):
         return rcopy(ret2.at[j], in2.at[j], r2_s.at[0], r2_r.at[j], at(b - 2, u))
 
+    def straight(j, place):
+        return rcopy(
+            ret2.at[j, :, rows(place), :], in2.at[j, :, rows(u), :],
+            r2_s.at[0], r2_r.at[j], at(0, place),
+        )
+
     def oq(k, j, place, dev):
         return rcopy(
             dqs.at[j, rows(place), :], dq_ref.at[:, cols((u * KH + j) * GD, GD)],
@@ -411,9 +452,16 @@
         def _():
             ret2[j] = acc2[j].astype(jnp.bfloat16)
 
-        @pl.when(has_down2)
+        to_alone = jnp.logical_and(b == 2, U == 2)
+
+        @pl.when(jnp.logical_and(has_down2, jnp.logical_not(to_alone)))
         def _():
             give2(j).start()
+
+        @pl.when(to_alone)
+        def _():
+            straight(j, u).start()
+            straight(j, 1 - u).start()
 
     def stage_b(j):
         @pl.when(even)
@@ -440,17 +488,139 @@
 
         return 0
 
-    lax.fori_loop(0, KH, head_step, 0)
-    if KH >= 2:
-        stage_b(KH - 2)
-    stage_b(KH - 1)
+    def alone_block(h, kc, vc, mask):
+        heads = [cols(h * GD + g * D, D) for g in range(GROUP)]
+        plane = h // KH
+        row = (h - plane * KH) * GROUP
+        weights, score_grads = [], []
+        for g in range(GROUP):
+            lse = stat_ref[plane, pl.ds(row + g, 1), :]
+            delta = stat_ref[plane, pl.ds(G + row + g, 1), :]
+            w = jnp.exp2(dot_nt(kc, q_ref[:, heads[g]]) * (scale * LOG2_E) - lse + mask)
+            ds = w * (dot_nt(vc, do_ref[:, heads[g]]) - delta)
+            score_grads.append(ds.astype(jnp.bfloat16))
+            weights.append(w.astype(jnp.bfloat16))
+        queries = jnp.concatenate([q_ref[:, c] for c in heads], axis=0)
+        cotangents = jnp.concatenate([do_ref[:, c] for c in heads], axis=0)
+        dv = dot_nn(jnp.concatenate(weights, axis=1), cotangents)
+        dk = dot_nn(jnp.concatenate(score_grads, axis=1), queries) * scale
+        return dk, dv, [dot_tn(ds, kc) * scale for ds in score_grads]
+
+    def alone_step(j, _):
+        for side in range(2):
+            plane = u if side == 0 else 1 - u
+            h = plane * KH + j
+            head = cols(h * D, D)
+            dk, dv, dq = alone_block(
+                h, kv_ref[0, :, head], kv_ref[1, :, head], bias[0, rows(u), rows(u)]
+            )
+            for g in range(GROUP):
+                dqt[:, g * D:(g + 1) * D] = dq[g]
+            if side == 0:
+                acc0[j, 0, rows(u), :] = dk
+                acc0[j, 1, rows(u), :] = dv
+            else:
+                loc1[j, 0] = dk
+                loc1[j, 1] = dv
+
+            @pl.when(u == 1)
+            def _():
+                if side == 0:
+                    near = cols(j * D, D)
+                    kc, vc = kvb[0, 0, rows(0), near], kvb[0, 1, rows(0), near]
+                else:
+                    kc, vc = kx[0, :, head], kx[1, :, head]
+                dk, dv, dq = alone_block(h, kc, vc, bias[0, rows(0), rows(1)])
+                for g in range(GROUP):
+                    dqt[:, g * D:(g + 1) * D] += dq[g]
+                if side == 0:
+                    acc0[j, 0, rows(0), :] = dk
+                    acc0[j, 1, rows(0), :] = dv
+                else:
+                    part[j, 0] = dk.astype(jnp.bfloat16)
+                    part[j, 1] = dv.astype(jnp.bfloat16)
+
+            if side == 0:
+                @pl.when(u == 0)
+                def _():
+                    acc0[j, :, rows(1), :] = jnp.zeros((2, T, D), jnp.float32)
+
+            dq_ref[:, cols(h * GD, GD)] = dqt[...].astype(jnp.bfloat16)
+        return 0
+
+    def alone_merge(j, _):
+        give1(j).wait_recv()
+        acc0[j] += in1[j].astype(jnp.float32)
+        dkvs[j] = acc0[j].astype(jnp.bfloat16)
+        okv(1, j, 1 - u, at(b, 1 - u)).start()
+        return 0
+
+    def alone_finish(j, _):
+        mine = cols((u * KH + j) * D, D)
+        other = cols(((1 - u) * KH + j) * D, D)
+
+        @pl.when(has_up2)
+        def _():
+            await_bytes(in2.at[j], r2_r.at[j])
+            acc0[j, :, rows(u), :] += in2[j, :, rows(u), :].astype(jnp.float32)
+            loc1[j] += in2[j, :, rows(1 - u), :].astype(jnp.float32)
+
+        dkv_ref[:, :, mine] = acc0[j, :, rows(u), :].astype(jnp.bfloat16)
+        dkv_ref[:, :, other] = (dkv_ref[:, :, other].astype(jnp.float32) + loc1[j]).astype(jnp.bfloat16)
+        return 0
+
+    @pl.when(grouped)
+    def _():
+        lax.fori_loop(0, KH, head_step, 0)
+        if KH >= 2:
+            stage_b(KH - 2)
+        stage_b(KH - 1)
+
+    if U == 2:
+        @pl.when(alone)
+        def _():
+            load_q.wait()
+            for j in range(3, KH):
+                forward(j)
+
+            @pl.when(u == 1)
+            def _():
+                kx_in().wait_recv()
+
+            lax.fori_loop(0, KH, alone_step, 0)
+
+            @pl.when(u == 1)
+            def _():
+                px_in().start()
+
+            @pl.when(u == 0)
+            def _():
+                px_in().wait_recv()
+                for j in range(KH):
+                    acc0[j, :, rows(0), :] += px[j].astype(jnp.float32)
+
+            lax.fori_loop(0, KH, alone_merge, 0)
+            await_bytes(dkv_ref.at[:, :, cols((1 - u) * KH * D, KH * D)], okv_r.at[0])
+            lax.fori_loop(0, KH, alone_finish, 0)
+
+            @pl.when(u == 0)
+            def _():
+                kx_in().wait_send()
+
+            @pl.when(u == 1)
+            def _():
+                px_in().wait_send()
 
     for k, to, _ in peers:
         id_in(k, u, at(b, to)).wait_send()
-        st_in(k, u, to, at(b, to)).wait_send()
         await_bytes(kv_ref.at[:, :, cols(to * KH * D, KH * D)], kv_s.at[k - 1])
-        for which in range(2):
-            await_bytes(qdb.at[which, rows(0), :], qd_s.at[which, k - 1])
+
+    @pl.when(grouped)
+    def _():
+        for k, to, _ in peers:
+            st_in(k, u, to, at(b, to)).wait_send()
+            for which in range(2):
+                await_bytes(qdb.at[which, rows(0), :], qd_s.at[which, k - 1])
 
     @pl.when(has_up2)
     def _():
@@ -470,11 +640,15 @@
     def _():
         await_bytes(ret2, r2_s.at[0])
 
-    for k, to, frm in peers:
-        await_bytes(dqs.at[:, rows(to), :], oq_s.at[k - 1])
+    for k, to, _ in peers:
         await_bytes(dkvs.at[:, :, rows(to), :], okv_s.at[k - 1])
-        await_bytes(dq_ref.at[:, cols(frm * KH * GD, KH * GD)], oq_r.at[k - 1])
-        await_bytes(dkv_ref.at[:, :, cols(frm * KH * D, KH * D)], okv_r.at[k - 1])
+
+    @pl.when(grouped)
+    def _():
+        for k, to, frm in peers:
+            await_bytes(dqs.at[:, rows(to), :], oq_s.at[k - 1])
+            await_bytes(dq_ref.at[:, cols(frm * KH * GD, KH * GD)], oq_r.at[k - 1])
+            await_bytes(dkv_ref.at[:, :, cols(frm * KH * D, KH * D)], okv_r.at[k - 1])
 
 
 def close_kernel(q_in, kv_in, q_out, k_out, v_out, sem):
@@ -499,6 +673,7 @@
     KH = KEY_VALUE_HEADS // U
     G = KH * GROUP
     D = HEAD_SIZE
+    GD = GROUP * D
     stat_rows = -(-2 * G // 8) * 8
     parts = lse_parts.transpose(1, 2, 0)
     ids = segment_ids.reshape(1, T)
@@ -541,8 +716,18 @@
             vm(parts.shape, f32),
             vm((1, T), jnp.int32),
             vm((U, stat_rows, T), f32),
+            vm(q.shape, bf),
+            vm((2, T, KH * D), bf),
+            vm((KH, 2, T, D), f32),
+            vm((KH, 2, T, D), bf),
+            vm((KH, 2, T, D), bf),
+            vm((T, GD), f32),
             dma((8,)),
             pltpu.SemaphoreType.REGULAR,
+            dma((1,)),
+            dma((1,)),
+            dma((1,)),
+            dma((1,)),
         ] + sems,
         compiler_params=pltpu.CompilerParams(
             collective_id=0, has_side_effects=True, vmem_limit_bytes=56 << 20

time: 35.4 us -> 37.8 us (1.068)
  Pallas kernels: 34.6 us -> 37.1 us
    pallas_call x1, Pallas kernels: 33.6 us -> 36.1 us  [per_device(): pl.pallas_call(functools.partial(kernel, U, B), out_shape=(vm(q.shape, bf...]
where the time goes in v3:
time: 37.8 us; the launch traced here: 37.7 us
  Pallas kernels  37.1 us (98%)
  between operations  0.64 us (2%)
    pallas_call x1, Pallas kernels, per_device(): pl.pallas_call(functools.partial(kernel, U, B), out_shape=(vm(q.shape, bf...  36.1 us
    pallas_call x1, Pallas kernels, per_device(): pl.pallas_call(close_kernel, out_shape=tuple((jax.ShapeDtypeStruct(r.shap...  1 us

profile of v3, /device:TPU:0, one launch (start us, length us, event | category | flops | bytes accessed | tf_op | source)
XLA Modules:
  0.0 37.7 jit_solution(16285144696903083663)
XLA Ops:
  0.6 36.1 %shard_map.94 = (bf16[128,2048]{1,0:T(8,128)(2,1)S(1)}, bf16[2,128,1024]{2,1,0:T(8,128)(2,1)S(1)}) custom-call(bf16[128,2048]{1,0:T(8,128)(2,1)} %q_hbm.1, bf16[128,2048]{1,0:T(8,128)(2,1)} %do_hbm.1, bf16[128,1024]{1,0:T(8,128)(2,1)} %k_hbm.1, bf16[128,1024]{1,0:T(8,128)(2,1)} %v_hbm.1, bf16[128,2048]{1,0:T(8,128)(2,1)} %out_hbm.1, f32[16,2,128]{2,1,0:T(2,128)} %bitcast.2, ...), custom_call_target="tpu_custom_call" | custom-call | tf_op jit(solution)/shard_map/pallas_call | solution.py:693
  36.7 1.0 %shard_map.95 = (bf16[128,2048]{1,0:T(8,128)(2,1)}, bf16[128,1024]{1,0:T(8,128)(2,1)}, bf16[128,1024]{1,0:T(8,128)(2,1)}) custom-call(bf16[128,2048]{1,0:T(8,128)(2,1)S(1)} %get-tuple-element.5.q_in, bf16[2,128,1024]{2,1,0:T(8,128)(2,1)S(1)} %get-tuple-element.6.kv_in), custom_call_target="tpu_custom_call" | custom-call | tf_op jit(solution)/shard_map/pallas_call | solution.py:737

commit v4 on v3

--- a/solution.py
+++ b/solution.py
@@ -234,15 +234,19 @@
         for j in range(1, KH):
             send_qd(j)
 
-    def kx_in():
-        return rcopy(kv_ref.at[:, :, pl.ds(0, KH * D)], kx, kx_s.at[0], kx_r.at[0], at(b, 1 - u))
-
-    def px_in():
-        return rcopy(part, px, px_s.at[0], px_r.at[0], at(b, 1 - u))
+    def kx_in(j):
+        head = cols(j * D, D)
+        return rcopy(
+            kv_ref.at[:, :, head], kx.at[:, :, head], kx_s.at[0], kx_r.at[j], at(b, 1 - u)
+        )
+
+    def px_in(j):
+        return rcopy(part.at[j], px.at[j], px_s.at[0], px_r.at[0], at(b, 1 - u))
 
     @pl.when(jnp.logical_and(alone, u == 0))
     def _():
-        kx_in().start()
+        for j in range(KH):
+            kx_in(j).start()
 
     @pl.when(jnp.logical_and(first, has_up2))
     def _():
@@ -482,7 +486,7 @@
     def head_step(j, _):
         compute(j)
 
-        @pl.when(j >= 2)
+        @pl.when(jnp.logical_and(j >= 2, b >= 2))
         def _():
             stage_b(jnp.maximum(j - 2, 0))
 
@@ -506,46 +510,49 @@
         dk = dot_nn(jnp.concatenate(score_grads, axis=1), queries) * scale
         return dk, dv, [dot_tn(ds, kc) * scale for ds in score_grads]
 
-    def alone_step(j, _):
+    def alone_own(j, _):
         for side in range(2):
-            plane = u if side == 0 else 1 - u
-            h = plane * KH + j
+            h = (u if side == 0 else 1 - u) * KH + j
             head = cols(h * D, D)
             dk, dv, dq = alone_block(
                 h, kv_ref[0, :, head], kv_ref[1, :, head], bias[0, rows(u), rows(u)]
             )
             for g in range(GROUP):
-                dqt[:, g * D:(g + 1) * D] = dq[g]
+                dqt[side, j, :, g * D:(g + 1) * D] = dq[g]
             if side == 0:
                 acc0[j, 0, rows(u), :] = dk
                 acc0[j, 1, rows(u), :] = dv
             else:
                 loc1[j, 0] = dk
                 loc1[j, 1] = dv
-
-            @pl.when(u == 1)
-            def _():
-                if side == 0:
-                    near = cols(j * D, D)
-                    kc, vc = kvb[0, 0, rows(0), near], kvb[0, 1, rows(0), near]
-                else:
-                    kc, vc = kx[0, :, head], kx[1, :, head]
-                dk, dv, dq = alone_block(h, kc, vc, bias[0, rows(0), rows(1)])
-                for g in range(GROUP):
-                    dqt[:, g * D:(g + 1) * D] += dq[g]
-                if side == 0:
-                    acc0[j, 0, rows(0), :] = dk
-                    acc0[j, 1, rows(0), :] = dv
-                else:
-                    part[j, 0] = dk.astype(jnp.bfloat16)
-                    part[j, 1] = dv.astype(jnp.bfloat16)
-
-            if side == 0:
-                @pl.when(u == 0)
-                def _():
-                    acc0[j, :, rows(1), :] = jnp.zeros((2, T, D), jnp.float32)
-
-            dq_ref[:, cols(h * GD, GD)] = dqt[...].astype(jnp.bfloat16)
+        return 0
+
+    def alone_store(j, _):
+        for side in range(2):
+            h = (u if side == 0 else 1 - u) * KH + j
+            dq_ref[:, cols(h * GD, GD)] = dqt[side, j].astype(jnp.bfloat16)
+        return 0
+
+    def alone_near(j, _):
+        head = cols(j * D, D)
+        dk, dv, dq = alone_block(
+            KH + j, kvb[0, 0, rows(0), head], kvb[0, 1, rows(0), head], bias[0, rows(0), rows(1)]
+        )
+        for g in range(GROUP):
+            dqt[0, j, :, g * D:(g + 1) * D] += dq[g]
+        acc0[j, 0, rows(0), :] = dk
+        acc0[j, 1, rows(0), :] = dv
+        return 0
+
+    def alone_far(j, _):
+        head = cols(j * D, D)
+        kx_in(j).wait_recv()
+        dk, dv, dq = alone_block(j, kx[0, :, head], kx[1, :, head], bias[0, rows(0), rows(1)])
+        part[j, 0] = dk.astype(jnp.bfloat16)
+        part[j, 1] = dv.astype(jnp.bfloat16)
+        px_in(j).start()
+        for g in range(GROUP):
+            dqt[1, j, :, g * D:(g + 1) * D] += dq[g]
         return 0
 
     def alone_merge(j, _):
@@ -572,44 +579,52 @@
     @pl.when(grouped)
     def _():
         lax.fori_loop(0, KH, head_step, 0)
-        if KH >= 2:
-            stage_b(KH - 2)
-        stage_b(KH - 1)
+        late = min(2, KH)
+
+        def last_step(j, _):
+            stage_b(j)
+            return 0
+
+        lax.fori_loop(jnp.where(first, 0, KH - late), KH, last_step, 0)
 
     if U == 2:
         @pl.when(alone)
         def _():
             load_q.wait()
+            alone_own(0, 0)
             for j in range(3, KH):
                 forward(j)
+            lax.fori_loop(1, KH, alone_own, 0)
+
+            @pl.when(u == 0)
+            def _():
+                for j in range(KH):
+                    acc0[j, :, rows(1), :] = jnp.zeros((2, T, D), jnp.float32)
 
             @pl.when(u == 1)
             def _():
-                kx_in().wait_recv()
-
-            lax.fori_loop(0, KH, alone_step, 0)
+                lax.fori_loop(0, KH, alone_near, 0)
+                lax.fori_loop(0, KH, alone_far, 0)
+
+            lax.fori_loop(0, KH, alone_merge, 0)
+            lax.fori_loop(0, KH, alone_store, 0)
+
+            @pl.when(u == 0)
+            def _():
+                await_bytes(px, px_r.at[0])
+                for j in range(KH):
+                    acc0[j, :, rows(0), :] += px[j].astype(jnp.float32)
+
+            await_bytes(dkv_ref.at[:, :, cols((1 - u) * KH * D, KH * D)], okv_r.at[0])
+            lax.fori_loop(0, KH, alone_finish, 0)
+
+            @pl.when(u == 0)
+            def _():
+                await_bytes(kx, kx_s.at[0])
 
             @pl.when(u == 1)
             def _():
-                px_in().start()
-
-            @pl.when(u == 0)
-            def _():
-                px_in().wait_recv()
-                for j in range(KH):
-                    acc0[j, :, rows(0), :] += px[j].astype(jnp.float32)
-
-            lax.fori_loop(0, KH, alone_merge, 0)
-            await_bytes(dkv_ref.at[:, :, cols((1 - u) * KH * D, KH * D)], okv_r.at[0])
-            lax.fori_loop(0, KH, alone_finish, 0)
-
-            @pl.when(u == 0)
-            def _():
-                kx_in().wait_send()
-
-            @pl.when(u == 1)
-            def _():
-                px_in().wait_send()
+                await_bytes(part, px_s.at[0])
 
     for k, to, _ in peers:
         id_in(k, u, at(b, to)).wait_send()
@@ -721,11 +736,11 @@
             vm((KH, 2, T, D), f32),
             vm((KH, 2, T, D), bf),
             vm((KH, 2, T, D), bf),
-            vm((T, GD), f32),
+            vm((2, KH, T, GD), f32),
             dma((8,)),
             pltpu.SemaphoreType.REGULAR,
             dma((1,)),
-            dma((1,)),
+            dma((KH,)),
             dma((1,)),
             dma((1,)),
         ] + sems,

time: 37.8 us -> 34.1 us (0.902)
  the two profiles are of different devices: /device:TPU:0 before, /device:TPU:2 now
where the time goes in v4:
time: 34.1 us; the launch traced here: 34 us
  Pallas kernels  33.4 us (98%)
  between operations  0.64 us (2%)
    pallas_call x1, Pallas kernels, per_device(): pl.pallas_call(functools.partial(kernel, U, B), out_shape=(vm(q.shape, bf...  32.4 us
    pallas_call x1, Pallas kernels, per_device(): pl.pallas_call(close_kernel, out_shape=tuple((jax.ShapeDtypeStruct(r.shap...  1 us

profile of v4, /device:TPU:2, one launch (start us, length us, event | category | flops | bytes accessed | tf_op | source)
XLA Modules:
  0.0 34.0 jit_solution(5976751980303799339)
XLA Ops:
  0.6 32.4 %shard_map.94 = (bf16[128,2048]{1,0:T(8,128)(2,1)S(1)}, bf16[2,128,1024]{2,1,0:T(8,128)(2,1)S(1)}) custom-call(bf16[128,2048]{1,0:T(8,128)(2,1)} %q_hbm.1, bf16[128,2048]{1,0:T(8,128)(2,1)} %do_hbm.1, bf16[128,1024]{1,0:T(8,128)(2,1)} %k_hbm.1, bf16[128,1024]{1,0:T(8,128)(2,1)} %v_hbm.1, bf16[128,2048]{1,0:T(8,128)(2,1)} %out_hbm.1, f32[16,2,128]{2,1,0:T(2,128)} %bitcast.2, ...), custom_call_target="tpu_custom_call" | custom-call | tf_op jit(solution)/shard_map/pallas_call | solution.py:708
  33.0 1.0 %shard_map.95 = (bf16[128,2048]{1,0:T(8,128)(2,1)}, bf16[128,1024]{1,0:T(8,128)(2,1)}, bf16[128,1024]{1,0:T(8,128)(2,1)}) custom-call(bf16[128,2048]{1,0:T(8,128)(2,1)S(1)} %get-tuple-element.5.q_in, bf16[2,128,1024]{2,1,0:T(8,128)(2,1)S(1)} %get-tuple-element.6.kv_in), custom_call_target="tpu_custom_call" | custom-call | tf_op jit(solution)/shard_map/pallas_call | solution.py:752

commit v5 on v4

--- a/solution.py
+++ b/solution.py
@@ -37,10 +37,10 @@
     dqacc, acc0, acc2, dqs, ret1, ret2, in1, in2, dkvs,
     do_ref, kv_ref, out_ref, lp_ref, ids_ref, stat_ref,
     q_ref, kx, loc1, part, px, dqt,
-    loc_sem, ready, kx_s, kx_r, px_s, px_r,
+    loc_sem, ready, relay,
     kv_s, kv_r, qd_s, qd_r, st_s, st_r, id_s, id_r,
     h2_s, h2_r, h2i_s, h2i_r, pt_s, pt_r, pti_s, pti_r,
-    r1_s, r1_r, r2_s, r2_r, oq_s, oq_r, okv_s, okv_r,
+    r1_s, r2_s, r2_r, oq_s, oq_r, okv_s, okv_r,
 ):
     U, B = uly_count, blk_count
     T = q_hbm.shape[0]
@@ -94,34 +94,44 @@
     first = b < 2
     alone = jnp.logical_and(b == 0, U == 2)
     grouped = jnp.logical_not(alone)
+    side_pair = lax.rem(b // 2, 2) == 1
+    has_up4 = b + 4 < B
     barrier = pltpu.get_barrier_semaphore()
+
+    def greet(sem, blk, uly):
+        pl.semaphore_signal(
+            sem, inc=1, device_id=at(blk, uly), device_id_type=pl.DeviceIdType.MESH
+        )
+
     for k in range(1, U):
-        pl.semaphore_signal(
-            barrier, inc=1, device_id=at(b, lax.rem(u + k, U)), device_id_type=pl.DeviceIdType.MESH
-        )
-    pl.semaphore_signal(barrier, inc=1, device_id=at(mate, u), device_id_type=pl.DeviceIdType.MESH)
-
-    @pl.when(has_up2)
-    def _():
-        pl.semaphore_signal(
-            barrier, inc=1, device_id=at(b + 2, u), device_id_type=pl.DeviceIdType.MESH
-        )
-
-    @pl.when(b >= 4)
-    def _():
-        pl.semaphore_signal(
-            barrier, inc=1, device_id=at(b - 2, u), device_id_type=pl.DeviceIdType.MESH
-        )
-
-    met_up2 = jnp.logical_and(has_up2, b >= 2)
-    expected = U + has_down2.astype(jnp.int32) + met_up2.astype(jnp.int32)
-    pl.semaphore_wait(barrier, expected)
-
-    @pl.when(jnp.logical_and(has_down2, b < 4))
-    def _():
-        pl.semaphore_signal(
-            ready, inc=1, device_id=at(b - 2, u), device_id_type=pl.DeviceIdType.MESH
-        )
+        greet(barrier, b, lax.rem(u + k, U))
+    greet(barrier, mate, u)
+    main_pair = jnp.logical_not(side_pair)
+    hub = u == 0
+    tree = u > 0
+
+    @pl.when(jnp.logical_and(jnp.logical_or(hub, main_pair), has_up2))
+    def _():
+        greet(barrier, b + 2, u)
+
+    @pl.when(jnp.logical_and(hub, has_down2))
+    def _():
+        greet(barrier, b - 2, u)
+
+    @pl.when(jnp.logical_and(jnp.logical_and(tree, main_pair), has_up4))
+    def _():
+        greet(barrier, b + 4, u)
+
+    met_up2 = jnp.logical_and(hub, has_up2)
+    pl.semaphore_wait(barrier, U + has_down2.astype(jnp.int32) + met_up2.astype(jnp.int32))
+
+    @pl.when(jnp.logical_and(tree, side_pair))
+    def _():
+        greet(ready, b - 2, u)
+
+    @pl.when(jnp.logical_and(jnp.logical_and(tree, main_pair), b >= 4))
+    def _():
+        greet(relay, b - 4, u)
 
     own_q = [
         load(src.at[:, cols(u * KH * GD, KH * GD)], qdb.at[i, rows(u), :], 6)
@@ -148,7 +158,7 @@
         return rcopy(
             ref.at[:, cols((peer * KH + j) * GD, GD)],
             qdb.at[which, rows(place), cols(j * GD, GD)],
-            qd_s.at[which, k - 1], qd_r.at[j, k - 1], dev,
+            qd_s.at[k - 1], qd_r.at[j, k - 1], dev,
         )
 
     def await_bytes(ref, sem):
@@ -161,12 +171,16 @@
         )
 
     peers = [(k, lax.rem(u + k, U), lax.rem(u + U - k, U)) for k in range(1, U)]
-    await_bytes(kvb.at[0, :, rows(u), :], loc_sem.at[0])
-
-    @pl.when(met_up2)
-    def _():
-        for j in range(KH):
-            h2(j, u).start()
+    soon = min(3, KH)
+
+    @pl.when(hub)
+    def _():
+        await_bytes(kvb.at[0, :, rows(u), :], loc_sem.at[0])
+
+        @pl.when(has_up2)
+        def _():
+            for j in range(soon):
+                h2(j, u).start()
 
     load_ids.wait()
     for k, to, _ in peers:
@@ -182,7 +196,7 @@
             for which in range(2):
                 qd_in(k, which, j, u, to, at(b, to)).start()
 
-    for j in range(min(2, KH)):
+    for j in range(soon):
         send_kv(j)
     own_id.start()
 
@@ -226,33 +240,50 @@
         for k, to, _ in peers:
             st_in(k, u, to, at(b, to)).start()
 
-    for j in range(2, KH):
+    for j in range(soon, KH):
         send_kv(j)
 
+    late_last = KH >= 3
+    holds_back = jnp.logical_and(odd == 1, b >= 2)
+
     @pl.when(grouped)
     def _():
-        for j in range(1, KH):
+        for j in range(1, KH - 1 if late_last else KH):
             send_qd(j)
+
+    if late_last:
+        @pl.when(jnp.logical_and(grouped, jnp.logical_not(holds_back)))
+        def _():
+            send_qd(KH - 1)
 
     def kx_in(j):
         head = cols(j * D, D)
         return rcopy(
-            kv_ref.at[:, :, head], kx.at[:, :, head], kx_s.at[0], kx_r.at[j], at(b, 1 - u)
+            kv_ref.at[:, :, head], kx.at[:, :, head], qd_s.at[0], qd_r.at[j, 0], at(b, 1 - u)
         )
 
     def px_in(j):
-        return rcopy(part.at[j], px.at[j], px_s.at[0], px_r.at[0], at(b, 1 - u))
+        return rcopy(part.at[j], px.at[j], qd_s.at[0], st_r.at[0], at(b, 1 - u))
 
     @pl.when(jnp.logical_and(alone, u == 0))
     def _():
         for j in range(KH):
             kx_in(j).start()
 
-    @pl.when(jnp.logical_and(first, has_up2))
-    def _():
-        pl.semaphore_wait(ready, 1)
-        for j in range(KH):
-            h2(j, u).start()
+    @pl.when(tree)
+    def _():
+        await_bytes(kvb.at[0, :, rows(u), :], loc_sem.at[0])
+
+        @pl.when(has_up2)
+        def _():
+            pl.semaphore_wait(ready, 1)
+            for j in range(soon):
+                h2(j, u).start()
+
+    @pl.when(jnp.logical_and(jnp.logical_and(tree, main_pair), has_up4))
+    def _():
+        pl.semaphore_wait(relay, 1)
+        greet(ready, b + 2, u)
 
     def h2id():
         return rcopy(idb.at[0], idb.at[2], h2i_s.at[0], h2i_r.at[0], at(b + 2, u))
@@ -307,6 +338,11 @@
     forward(0)
     if KH > 1:
         forward(1)
+
+    @pl.when(has_up2)
+    def _():
+        for j in range(soon, KH):
+            h2(j, u).start()
 
     @pl.when(has_down2)
     def _():
@@ -392,10 +428,16 @@
             lax.fori_loop(0, steps, key_step, 0)
 
     def give1(j):
-        return rcopy(ret1.at[j], in1.at[j], r1_s.at[0], r1_r.at[j], at(mate, u))
+        return rcopy(ret1.at[j], in1.at[j], r1_s.at[0], kv_r.at[j, 0], at(mate, u))
 
     def give2(j):
         return rcopy(ret2.at[j], in2.at[j], r2_s.at[0], r2_r.at[j], at(b - 2, u))
+
+    def give2_part(which):
+        return rcopy(
+            ret2.at[KH - 1, which], in2.at[KH - 1, which],
+            r2_s.at[0], r2_r.at[KH - 1 + which], at(b - 2, u),
+        )
 
     def straight(j, place):
         return rcopy(
@@ -415,6 +457,10 @@
             okv_s.at[k - 1], okv_r.at[k - 1], dev,
         )
 
+    def send_oq(j):
+        for k, to, _ in peers:
+            oq(k, j, to, at(b, to)).start()
+
     def compute(j):
         for k, _, frm in peers:
             await_bytes(qdb.at[:, rows(frm), cols(j * GD, GD)], qd_r.at[j, k - 1])
@@ -438,13 +484,30 @@
         def _():
             hop_grads(2, j, acc2)
 
-        stage_a(j)
+        @pl.when(even)
+        def _():
+            stage_a(j)
+
         hop_grads(0, j, acc0)
 
         dqs[j] = (dqacc[...] * scale).astype(jnp.bfloat16)
-        for k, to, _ in peers:
-            oq(k, j, to, at(b, to)).start()
+        if late_last:
+            @pl.when(jnp.logical_and(holds_back, j == KH - 3))
+            def _():
+                send_qd(KH - 1)
+                for i in range(KH - 3):
+                    send_oq(i)
+
+            @pl.when(jnp.logical_or(jnp.logical_not(holds_back), j >= KH - 3))
+            def _():
+                send_oq(j)
+        else:
+            send_oq(j)
         dq_ref[:, cols((u * KH + j) * GD, GD)] = dqs[j, rows(u), :]
+
+        @pl.when(odd == 1)
+        def _():
+            stage_a(j)
 
     def stage_a(j):
         @pl.when(jnp.logical_and(odd == 1, has_down2))
@@ -458,9 +521,16 @@
 
         to_alone = jnp.logical_and(b == 2, U == 2)
 
-        @pl.when(jnp.logical_and(has_down2, jnp.logical_not(to_alone)))
+        to_grouped = jnp.logical_and(has_down2, jnp.logical_not(to_alone))
+
+        @pl.when(jnp.logical_and(to_grouped, j < KH - 1))
         def _():
             give2(j).start()
+
+        @pl.when(jnp.logical_and(to_grouped, j == KH - 1))
+        def _():
+            for which in range(2):
+                give2_part(which).start()
 
         @pl.when(to_alone)
         def _():
@@ -482,6 +552,29 @@
         for k, to, _ in peers:
             okv(k, j, to, at(b, to)).start()
         dkv_ref[:, :, cols((u * KH + j) * D, D)] = dkvs[j, :, rows(u), :]
+
+    def stage_b_last():
+        j = KH - 1
+
+        @pl.when(even)
+        def _():
+            give1(j).wait_recv()
+            acc0[j] += in1[j].astype(jnp.float32)
+
+        for which in range(2):
+            @pl.when(has_up2)
+            def _():
+                give2_part(which).wait_recv()
+                acc0[j, which] += in2[j, which].astype(jnp.float32)
+
+            dkvs[j, which] = acc0[j, which].astype(jnp.bfloat16)
+            head = cols((u * KH + j) * D, D)
+            for k, to, _ in peers:
+                rcopy(
+                    dkvs.at[j, which, rows(to), :], dkv_ref.at[which, :, head],
+                    okv_s.at[k - 1], okv_r.at[k - 1], at(b, to),
+                ).start()
+            dkv_ref[which, :, head] = dkvs[j, which, rows(u), :]
 
     def head_step(j, _):
         compute(j)
@@ -585,7 +678,8 @@
             stage_b(j)
             return 0
 
-        lax.fori_loop(jnp.where(first, 0, KH - late), KH, last_step, 0)
+        lax.fori_loop(jnp.where(first, 0, KH - late), KH - 1, last_step, 0)
+        stage_b_last()
 
     if U == 2:
         @pl.when(alone)
@@ -611,7 +705,7 @@
 
             @pl.when(u == 0)
             def _():
-                await_bytes(px, px_r.at[0])
+                await_bytes(px, st_r.at[0])
                 for j in range(KH):
                     acc0[j, :, rows(0), :] += px[j].astype(jnp.float32)
 
@@ -620,11 +714,11 @@
 
             @pl.when(u == 0)
             def _():
-                await_bytes(kx, kx_s.at[0])
+                await_bytes(kx, qd_s.at[0])
 
             @pl.when(u == 1)
             def _():
-                await_bytes(part, px_s.at[0])
+                await_bytes(part, qd_s.at[0])
 
     for k, to, _ in peers:
         id_in(k, u, at(b, to)).wait_send()
@@ -634,8 +728,7 @@
     def _():
         for k, to, _ in peers:
             st_in(k, u, to, at(b, to)).wait_send()
-            for which in range(2):
-                await_bytes(qdb.at[which, rows(0), :], qd_s.at[which, k - 1])
+            await_bytes(qdb.at[:, rows(0), :], qd_s.at[k - 1])
 
     @pl.when(has_up2)
     def _():
@@ -697,11 +790,11 @@
     dma = pltpu.SemaphoreType.DMA
     sems = []
     for send, recv in [
-        ((n,), (KH, n)), ((2, n), (KH, n)), ((n,), (n,)), ((n,), (n,)),
+        ((n,), (KH, n)), ((n,), (KH, n)), ((n,), (n,)), ((n,), (n,)),
         ((1,), (KH,)), ((1,), (1,)), ((1,), (KH,)), ((1,), (1,)),
-        ((1,), (KH,)), ((1,), (KH,)), ((n,), (n,)), ((n,), (n,)),
+        ((1,), None), ((1,), (KH + 1,)), ((n,), (n,)), ((n,), (n,)),
     ]:
-        sems += [dma(send), dma(recv)]
+        sems += [dma(shape) for shape in (send, recv) if shape is not None]
     vm = pltpu.VMEM
     in_vmem = pl.BlockSpec(memory_space=pltpu.VMEM)
     in_hbm = pl.BlockSpec(memory_space=pltpu.HBM)
@@ -739,10 +832,7 @@
             vm((2, KH, T, GD), f32),
             dma((8,)),
             pltpu.SemaphoreType.REGULAR,
-            dma((1,)),
-            dma((KH,)),
-            dma((1,)),
-            dma((1,)),
+            pltpu.SemaphoreType.REGULAR,
         ] + sems,
         compiler_params=pltpu.CompilerParams(
             collective_id=0, has_side_effects=True, vmem_limit_bytes=56 << 20

time: 34.1 us -> 34 us (level)
  Pallas kernels: 33.4 us -> 33 us
    pallas_call x1, Pallas kernels: 32.4 us -> 32 us  [per_device(): pl.pallas_call(functools.partial(kernel, U, B), out_shape=(vm(q.shape, bf...]
where the time goes in v5:
time: 34 us; the launch traced here: 33.6 us
  Pallas kernels  33 us (97%)
  between operations  0.64 us (2%)
    pallas_call x1, Pallas kernels, per_device(): pl.pallas_call(functools.partial(kernel, U, B), out_shape=(vm(q.shape, bf...  32 us
    pallas_call x1, Pallas kernels, per_device(): pl.pallas_call(close_kernel, out_shape=tuple((jax.ShapeDtypeStruct(r.shap...  1 us

profile of v5, /device:TPU:2, one launch (start us, length us, event | category | flops | bytes accessed | tf_op | source)
XLA Modules:
  0.0 33.6 jit_solution(7934119494119141879)
XLA Ops:
  0.6 32.0 %shard_map.94 = (bf16[128,2048]{1,0:T(8,128)(2,1)S(1)}, bf16[2,128,1024]{2,1,0:T(8,128)(2,1)S(1)}) custom-call(bf16[128,2048]{1,0:T(8,128)(2,1)} %q_hbm.1, bf16[128,2048]{1,0:T(8,128)(2,1)} %do_hbm.1, bf16[128,1024]{1,0:T(8,128)(2,1)} %k_hbm.1, bf16[128,1024]{1,0:T(8,128)(2,1)} %v_hbm.1, bf16[128,2048]{1,0:T(8,128)(2,1)} %out_hbm.1, f32[16,2,128]{2,1,0:T(2,128)} %bitcast.2, ...), custom_call_target="tpu_custom_call" | custom-call | tf_op jit(solution)/shard_map/pallas_call | solution.py:801
  32.6 1.0 %shard_map.95 = (bf16[128,2048]{1,0:T(8,128)(2,1)}, bf16[128,1024]{1,0:T(8,128)(2,1)}, bf16[128,1024]{1,0:T(8,128)(2,1)}) custom-call(bf16[128,2048]{1,0:T(8,128)(2,1)S(1)} %get-tuple-element.5.q_in, bf16[2,128,1024]{2,1,0:T(8,128)(2,1)S(1)} %get-tuple-element.6.kv_in), custom_call_target="tpu_custom_call" | custom-call | tf_op jit(solution)/shard_map/pallas_call | solution.py:842

commit v6 on v5

--- a/solution.py
+++ b/solution.py
@@ -84,11 +84,16 @@
         for i, src in enumerate((k_hbm, v_hbm))
     ]
     load_ids = load(ids_hbm, ids_ref, 1)
-    load_kv = [load(src, kv_ref.at[i], 2) for i, src in enumerate((k_hbm, v_hbm))]
+    load_kv = [
+        load(src.at[:, part], kv_ref.at[i, :, part], 2 if k else 0)
+        for k in list(range(1, U)) + [0]
+        for part in [cols(lax.rem(u + k, U) * KH * D, KH * D)]
+        for i, src in enumerate((k_hbm, v_hbm))
+    ]
     load_do = load(do_hbm, do_ref, 3)
     load_out = load(out_hbm, out_ref, 4)
     load_lp = load(lp_hbm, lp_ref, 5)
-    for copy in load_kv + [load_ids] + own_kv + [load_do, load_out, load_lp]:
+    for copy in [load_ids] + load_kv + own_kv + [load_do, load_out, load_lp]:
         copy.start()
 
     first = b < 2
@@ -175,7 +180,7 @@
 
     @pl.when(hub)
     def _():
-        await_bytes(kvb.at[0, :, rows(u), :], loc_sem.at[0])
+        await_bytes(kv_ref.at[:, :, pl.ds(0, min(2, U) * KH * D)], loc_sem.at[0])
 
         @pl.when(has_up2)
         def _():
@@ -185,7 +190,8 @@
     load_ids.wait()
     for k, to, _ in peers:
         id_in(k, u, at(b, to)).start()
-    await_bytes(kv_ref, loc_sem.at[2])
+    if U > 1:
+        await_bytes(kv_ref.at[:, :, pl.ds(0, (U - 1) * KH * D)], loc_sem.at[2])
 
     def send_kv(j):
         for k, to, _ in peers:
@@ -243,18 +249,10 @@
     for j in range(soon, KH):
         send_kv(j)
 
-    late_last = KH >= 3
-    holds_back = jnp.logical_and(odd == 1, b >= 2)
-
     @pl.when(grouped)
     def _():
-        for j in range(1, KH - 1 if late_last else KH):
+        for j in range(1, KH):
             send_qd(j)
-
-    if late_last:
-        @pl.when(jnp.logical_and(grouped, jnp.logical_not(holds_back)))
-        def _():
-            send_qd(KH - 1)
 
     def kx_in(j):
         head = cols(j * D, D)
@@ -272,7 +270,7 @@
 
     @pl.when(tree)
     def _():
-        await_bytes(kvb.at[0, :, rows(u), :], loc_sem.at[0])
+        await_bytes(kv_ref.at[:, :, pl.ds(0, min(2, U) * KH * D)], loc_sem.at[0])
 
         @pl.when(has_up2)
         def _():
@@ -457,10 +455,6 @@
             okv_s.at[k - 1], okv_r.at[k - 1], dev,
         )
 
-    def send_oq(j):
-        for k, to, _ in peers:
-            oq(k, j, to, at(b, to)).start()
-
     def compute(j):
         for k, _, frm in peers:
             await_bytes(qdb.at[:, rows(frm), cols(j * GD, GD)], qd_r.at[j, k - 1])
@@ -491,18 +485,8 @@
         hop_grads(0, j, acc0)
 
         dqs[j] = (dqacc[...] * scale).astype(jnp.bfloat16)
-        if late_last:
-            @pl.when(jnp.logical_and(holds_back, j == KH - 3))
-            def _():
-                send_qd(KH - 1)
-                for i in range(KH - 3):
-                    send_oq(i)
-
-            @pl.when(jnp.logical_or(jnp.logical_not(holds_back), j >= KH - 3))
-            def _():
-                send_oq(j)
-        else:
-            send_oq(j)
+        for k, to, _ in peers:
+            oq(k, j, to, at(b, to)).start()
         dq_ref[:, cols((u * KH + j) * GD, GD)] = dqs[j, rows(u), :]
 
         @pl.when(odd == 1)

time: 34 us -> 33.7 us (level)
  no operation moved by 1% of the time
where the time goes in v6:
time: 33.7 us; the launch traced here: 33.6 us
  Pallas kernels  32.9 us (98%)
  between operations  0.64 us (2%)
    pallas_call x1, Pallas kernels, per_device(): pl.pallas_call(functools.partial(kernel, U, B), out_shape=(vm(q.shape, bf...  31.9 us
    pallas_call x1, Pallas kernels, per_device(): pl.pallas_call(close_kernel, out_shape=tuple((jax.ShapeDtypeStruct(r.shap...  1 us

profile of v6, /device:TPU:2, one launch (start us, length us, event | category | flops | bytes accessed | tf_op | source)
XLA Modules:
  0.0 33.6 jit_solution(13262814184493589284)
XLA Ops:
  0.6 31.9 %shard_map.94 = (bf16[128,2048]{1,0:T(8,128)(2,1)S(1)}, bf16[2,128,1024]{2,1,0:T(8,128)(2,1)S(1)}) custom-call(bf16[128,2048]{1,0:T(8,128)(2,1)} %q_hbm.1, bf16[128,2048]{1,0:T(8,128)(2,1)} %do_hbm.1, bf16[128,1024]{1,0:T(8,128)(2,1)} %k_hbm.1, bf16[128,1024]{1,0:T(8,128)(2,1)} %v_hbm.1, bf16[128,2048]{1,0:T(8,128)(2,1)} %out_hbm.1, f32[16,2,128]{2,1,0:T(2,128)} %bitcast.2, ...), custom_call_target="tpu_custom_call" | custom-call | tf_op jit(solution)/shard_map/pallas_call | solution.py:785
  32.6 1.0 %shard_map.95 = (bf16[128,2048]{1,0:T(8,128)(2,1)}, bf16[128,1024]{1,0:T(8,128)(2,1)}, bf16[128,1024]{1,0:T(8,128)(2,1)}) custom-call(bf16[128,2048]{1,0:T(8,128)(2,1)S(1)} %get-tuple-element.5.q_in, bf16[2,128,1024]{2,1,0:T(8,128)(2,1)S(1)} %get-tuple-element.6.kv_in), custom_call_target="tpu_custom_call" | custom-call | tf_op jit(solution)/shard_map/pallas_call | solution.py:826

commit v7 on v6

--- a/solution.py
+++ b/solution.py
@@ -202,7 +202,7 @@
             for which in range(2):
                 qd_in(k, which, j, u, to, at(b, to)).start()
 
-    for j in range(soon):
+    for j in range(KH):
         send_kv(j)
     own_id.start()
 
@@ -246,8 +246,6 @@
         for k, to, _ in peers:
             st_in(k, u, to, at(b, to)).start()
 
-    for j in range(soon, KH):
-        send_kv(j)
 
     @pl.when(grouped)
     def _():
@@ -371,8 +369,8 @@
         for k, _, frm in peers:
             st_in(k, frm, frm, at(b, frm)).wait_recv()
 
-    if KH > 2:
-        forward(2)
+    for j in range(2, KH):
+        forward(j)
     arrive2(0)
 
     tile = min(TILE, R)
@@ -466,10 +464,6 @@
             hop_grads(1, j, ret1)
             give1(j).start()
 
-        @pl.when(j + 3 < KH)
-        def _():
-            forward(jnp.minimum(j + 3, KH - 1))
-
         @pl.when(j + 1 < KH)
         def _():
             arrive2(jnp.minimum(j + 1, KH - 1))
@@ -562,11 +556,6 @@
 
     def head_step(j, _):
         compute(j)
-
-        @pl.when(jnp.logical_and(j >= 2, b >= 2))
-        def _():
-            stage_b(jnp.maximum(j - 2, 0))
-
         return 0
 
     def alone_block(h, kc, vc, mask):
@@ -656,23 +645,19 @@
     @pl.when(grouped)
     def _():
         lax.fori_loop(0, KH, head_step, 0)
-        late = min(2, KH)
 
         def last_step(j, _):
             stage_b(j)
             return 0
 
-        lax.fori_loop(jnp.where(first, 0, KH - late), KH - 1, last_step, 0)
+        lax.fori_loop(0, KH - 1, last_step, 0)
         stage_b_last()
 
     if U == 2:
         @pl.when(alone)
         def _():
             load_q.wait()
-            alone_own(0, 0)
-            for j in range(3, KH):
-                forward(j)
-            lax.fori_loop(1, KH, alone_own, 0)
+            lax.fori_loop(0, KH, alone_own, 0)
 
             @pl.when(u == 0)
             def _():

time: 33.7 us -> 33.7 us (level)
  no operation moved by 1% of the time
where the time goes in v7:
time: 33.7 us; the launch traced here: 33.6 us
  Pallas kernels  32.9 us (98%)
  between operations  0.64 us (2%)
    pallas_call x1, Pallas kernels, per_device(): pl.pallas_call(functools.partial(kernel, U, B), out_shape=(vm(q.shape, bf...  31.9 us
    pallas_call x1, Pallas kernels, per_device(): pl.pallas_call(close_kernel, out_shape=tuple((jax.ShapeDtypeStruct(r.shap...  1 us

profile of v7, /device:TPU:2, one launch (start us, length us, event | category | flops | bytes accessed | tf_op | source)
XLA Modules:
  0.0 33.6 jit_solution(9502646793372734889)
XLA Ops:
  0.6 31.9 %shard_map.94 = (bf16[128,2048]{1,0:T(8,128)(2,1)S(1)}, bf16[2,128,1024]{2,1,0:T(8,128)(2,1)S(1)}) custom-call(bf16[128,2048]{1,0:T(8,128)(2,1)} %q_hbm.1, bf16[128,2048]{1,0:T(8,128)(2,1)} %do_hbm.1, bf16[128,1024]{1,0:T(8,128)(2,1)} %k_hbm.1, bf16[128,1024]{1,0:T(8,128)(2,1)} %v_hbm.1, bf16[128,2048]{1,0:T(8,128)(2,1)} %out_hbm.1, f32[16,2,128]{2,1,0:T(2,128)} %bitcast.2, ...), custom_call_target="tpu_custom_call" | custom-call | tf_op jit(solution)/shard_map/pallas_call | solution.py:770
  32.6 1.0 %shard_map.95 = (bf16[128,2048]{1,0:T(8,128)(2,1)}, bf16[128,1024]{1,0:T(8,128)(2,1)}, bf16[128,1024]{1,0:T(8,128)(2,1)}) custom-call(bf16[128,2048]{1,0:T(8,128)(2,1)S(1)} %get-tuple-element.5.q_in, bf16[2,128,1024]{2,1,0:T(8,128)(2,1)S(1)} %get-tuple-element.6.kv_in), custom_call_target="tpu_custom_call" | custom-call | tf_op jit(solution)/shard_map/pallas_call | solution.py:811

commit v8 on v7

--- a/solution.py
+++ b/solution.py
@@ -84,16 +84,20 @@
         for i, src in enumerate((k_hbm, v_hbm))
     ]
     load_ids = load(ids_hbm, ids_ref, 1)
+    others = list(range(1, U))
     load_kv = [
-        load(src.at[:, part], kv_ref.at[i, :, part], 2 if k else 0)
-        for k in list(range(1, U)) + [0]
-        for part in [cols(lax.rem(u + k, U) * KH * D, KH * D)]
+        load(src.at[:, part], kv_ref.at[i, :, part], sem)
+        for sem, places, head, count in [
+            (8, others, 0, 1), (2, others if KH > 1 else [], 1, KH - 1), (0, [0], 0, KH)
+        ]
+        for k in places
+        for part in [cols((lax.rem(u + k, U) * KH + head) * D, count * D)]
         for i, src in enumerate((k_hbm, v_hbm))
     ]
     load_do = load(do_hbm, do_ref, 3)
     load_out = load(out_hbm, out_ref, 4)
     load_lp = load(lp_hbm, lp_ref, 5)
-    for copy in [load_ids] + load_kv + own_kv + [load_do, load_out, load_lp]:
+    for copy in load_kv[:2 * (U - 1)] + [load_ids] + load_kv[2 * (U - 1):] + own_kv + [load_do, load_out, load_lp]:
         copy.start()
 
     first = b < 2
@@ -187,12 +191,6 @@
             for j in range(soon):
                 h2(j, u).start()
 
-    load_ids.wait()
-    for k, to, _ in peers:
-        id_in(k, u, at(b, to)).start()
-    if U > 1:
-        await_bytes(kv_ref.at[:, :, pl.ds(0, (U - 1) * KH * D)], loc_sem.at[2])
-
     def send_kv(j):
         for k, to, _ in peers:
             kv_in(k, j, u, to, at(b, to)).start()
@@ -202,7 +200,15 @@
             for which in range(2):
                 qd_in(k, which, j, u, to, at(b, to)).start()
 
-    for j in range(KH):
+    if U > 1:
+        await_bytes(kv_ref.at[:, :, pl.ds(0, (U - 1) * D)], loc_sem.at[8])
+    send_kv(0)
+    load_ids.wait()
+    for k, to, _ in peers:
+        id_in(k, u, at(b, to)).start()
+    if U > 1 and KH > 1:
+        await_bytes(kv_ref.at[:, :, pl.ds(0, (U - 1) * (KH - 1) * D)], loc_sem.at[2])
+    for j in range(1, KH):
         send_kv(j)
     own_id.start()
 
@@ -799,7 +805,7 @@
             vm((KH, 2, T, D), bf),
             vm((KH, 2, T, D), bf),
             vm((2, KH, T, GD), f32),
-            dma((8,)),
+            dma((9,)),
             pltpu.SemaphoreType.REGULAR,
             pltpu.SemaphoreType.REGULAR,
         ] + sems,

time: 33.7 us -> 33.7 us (level)
  no operation moved by 1% of the time
where the time goes in v8:
time: 33.7 us; the launch traced here: 33.6 us
  Pallas kernels  32.9 us (98%)
  between operations  0.64 us (2%)
    pallas_call x1, Pallas kernels, per_device(): pl.pallas_call(functools.partial(kernel, U, B), out_shape=(vm(q.shape, bf...  31.9 us
    pallas_call x1, Pallas kernels, per_device(): pl.pallas_call(close_kernel, out_shape=tuple((jax.ShapeDtypeStruct(r.shap...  1 us

profile of v8, /device:TPU:2, one launch (start us, length us, event | category | flops | bytes accessed | tf_op | source)
XLA Modules:
  0.0 33.6 jit_solution(2572215038213238554)
XLA Ops:
  0.6 31.9 %shard_map.94 = (bf16[128,2048]{1,0:T(8,128)(2,1)S(1)}, bf16[2,128,1024]{2,1,0:T(8,128)(2,1)S(1)}) custom-call(bf16[128,2048]{1,0:T(8,128)(2,1)} %q_hbm.1, bf16[128,2048]{1,0:T(8,128)(2,1)} %do_hbm.1, bf16[128,1024]{1,0:T(8,128)(2,1)} %k_hbm.1, bf16[128,1024]{1,0:T(8,128)(2,1)} %v_hbm.1, bf16[128,2048]{1,0:T(8,128)(2,1)} %out_hbm.1, f32[16,2,128]{2,1,0:T(2,128)} %bitcast.2, ...), custom_call_target="tpu_custom_call" | custom-call | tf_op jit(solution)/shard_map/pallas_call | solution.py:776
  32.6 1.0 %shard_map.95 = (bf16[128,2048]{1,0:T(8,128)(2,1)}, bf16[128,1024]{1,0:T(8,128)(2,1)}, bf16[128,1024]{1,0:T(8,128)(2,1)}) custom-call(bf16[128,2048]{1,0:T(8,128)(2,1)S(1)} %get-tuple-element.5.q_in, bf16[2,128,1024]{2,1,0:T(8,128)(2,1)S(1)} %get-tuple-element.6.kv_in), custom_call_target="tpu_custom_call" | custom-call | tf_op jit(solution)/shard_map/pallas_call | solution.py:817
